TPU v7x, 256 devices: a whole 4x4x8 slice. The times are simulated.
256 devices in a mesh: grid: 32 (over z, y), atom: 8 (over x, core).
Axes of the slice: x: 4, y: 4, z: 8, core: 2. Of those that a mesh axis runs over, the one named last changes fastest.
Arguments:
- weights: float32 [4194304], P(('grid', 'atom')), may hold values from 0.25 to 4
- target: float32 [4194304], P(('grid', 'atom')), may hold values from -6 to 6
- coupling: float32 [4194304], P(('grid', 'atom')), may hold values from -0.9 to 0.9
- multipole_basis: float32 [25, 4194304], P(None, ('grid', 'atom')), may hold values from -6 to 6
- rho_hist: float32 [8, 4194304], P(None, ('grid', 'atom')), may hold values from -6 to 6
- res_hist: float32 [8, 4194304], P(None, ('grid', 'atom')), may hold values from -6 to 6
- batch_atom: int32 [16384], P(('grid', 'atom')), may hold values from 0 to 4095
- owner_slot: int32 [4096], replicated, may hold values from 0 to 4095, each once
- slot_index: int32 [2], replicated, may hold values from 0 to 7
Outputs:
- density: float32 [4194304], P(('grid', 'atom'))
- moments: float32 [25, 4096], P(None, 'atom')
Inputs may be any that keep to these rules, and one draw needn't show every extreme that they name: `owner_slot`: each slot 0 to 4095 belongs to exactly one atom.
All inputs are finite; a program needn't handle non-finite values.
Results may differ from a plain program's by a relative error of at most 0.00011.
Values sent between devices are 32-bit elements; how exact they have to be, the bound alone decides.
A program may use at most 64 MiB of HBM per device.

v0:
```python
import functools
import math

import jax
import jax.numpy as jnp
from jax import lax
from jax.experimental import pallas as pl
from jax.experimental.pallas import tpu as pltpu
from jax.sharding import PartitionSpec as P

MESH = pl.DeviceIdType.MESH
LANES = 128
SUBS = 8
mixing_beta = 0.5
ridge_share = 0.1
F32 = jnp.float32


def solve_coeffs(entry, hist_len):
    trace = entry[0][0]
    for i in range(1, hist_len):
        trace = trace + entry[i][i]
    ridge = (ridge_share / hist_len) * trace
    low = [[entry[i][j] for j in range(i + 1)] for i in range(hist_len)]
    for i in range(hist_len):
        low[i][i] = low[i][i] + ridge
    inverse = [None] * hist_len
    factor = [[None] * hist_len for _ in range(hist_len)]
    forward = [jnp.ones_like(trace) for _ in range(hist_len)]
    for j in range(hist_len):
        inverse[j] = 1.0 / low[j][j]
        for i in range(j + 1, hist_len):
            factor[i][j] = low[i][j] * inverse[j]
        for i in range(j + 1, hist_len):
            forward[i] = forward[i] - factor[i][j] * forward[j]
            for k in range(j + 1, i + 1):
                low[i][k] = low[i][k] - factor[i][j] * low[k][j]
    backward = [forward[i] * inverse[i] for i in range(hist_len)]
    for j in reversed(range(hist_len)):
        for i in range(j):
            backward[i] = backward[i] - factor[j][i] * backward[j]
    total = backward[0]
    for i in range(1, hist_len):
        total = total + backward[i]
    return [backward[i] / total for i in range(hist_len)]


def split(x):
    pieces = []
    for _ in range(3):
        piece = x.astype(jnp.bfloat16).astype(F32)
        pieces.append(piece)
        x = x - piece
    return pieces


def kernel(
    cfg,
    batch_atom,
    owner_slot,
    slot_index,
    w_hbm,
    target_hbm,
    coupling_hbm,
    basis_hbm,
    rho_hbm,
    res_hbm,
    density_out,
    moments_out,
    w,
    target,
    coupling,
    basis,
    rho,
    res,
    fresh,
    fresh_w,
    row_bufs,
    moment_bufs,
    near,
    own,
    hist_moments,
    base_rows,
    correct,
    load_sem,
    send_sem,
    recv_sem,
):
    iters, hist_len, harmonics, batches, width, owned, groups, members, scale = cfg
    devices = groups * members
    tiles = w.shape[0]
    per_batch = width // LANES
    half = LANES // 2
    rows = batches // 4
    my_group = lax.axis_index("grid")
    my_member = lax.axis_index("atom")
    me = my_group * members + my_member

    def peer(step):
        spot = lax.rem(me + step, devices)
        return spot, (lax.div(spot, members), lax.rem(spot, members))

    barrier = pltpu.get_barrier_semaphore()

    @pl.loop(1, devices)
    def _(step):
        pl.semaphore_signal(barrier, inc=1, device_id=peer(step)[1], device_id_type=MESH)

    loads = [
        pltpu.make_async_copy(src, dst, load_sem.at[k])
        for k, (src, dst) in enumerate(
            ((res_hbm, res), (w_hbm, w), (basis_hbm, basis), (rho_hbm, rho), (target_hbm, target), (coupling_hbm, coupling))
        )
    ]
    for load in loads:
        load.start()

    lane = lax.broadcasted_iota(jnp.int32, (SUBS, LANES), 1)
    sub = lax.broadcasted_iota(jnp.int32, (SUBS, LANES), 0)
    quarter = lane // 32
    lane_row = lax.broadcasted_iota(jnp.int32, (1, LANES), 1)

    slot_row = jnp.zeros((1, LANES), F32)
    slot_cols = []
    for block in range(batches // SUBS):
        col = jnp.zeros((SUBS, LANES), F32)
        for at in range(SUBS):
            b = block * SUBS + at
            slot = owner_slot[batch_atom[b]].astype(F32)
            slot_row = jnp.where(lane_row == half + b, slot, slot_row)
            col = jnp.where(sub == at, slot, col)
        slot_cols.append(col)
    slot_col = jnp.concatenate(slot_cols, axis=0)

    def lane_tile(t):
        return pl.ds(pl.multiple_of(t * LANES, LANES), LANES)

    def exchange(buf, which):
        def copy(step, spot):
            dst, device = peer(step)
            return pltpu.make_async_remote_copy(
                src_ref=buf.at[me],
                dst_ref=buf.at[spot],
                send_sem=send_sem.at[which, step],
                recv_sem=recv_sem.at[which, spot],
                device_id=device,
                device_id_type=MESH,
            )

        @pl.loop(1, devices)
        def _(step):
            copy(step, me).start()

        def wait():
            @pl.loop(1, devices)
            def _(step):
                copy(step, lax.rem(me - step + devices, devices)).wait_recv()

            @pl.loop(1, devices)
            def _(step):
                copy(step, me).wait_send()

        return wait

    def total_row(buf):
        total = buf[0]
        for spot in range(1, devices):
            total = total + buf[spot]
        return total

    def splat(row, k):
        return jnp.broadcast_to(row[:, k : k + 1], (1, LANES))

    shifts = hist_len // 2 + 1
    entry = None
    for iteration in range(iters):
        row_buf = row_bufs.at[iteration]
        moment_buf = moment_bufs.at[iteration]
        last = iteration == iters - 1

        if iteration == 0:
            loads[0].wait()
            loads[1].wait()

            def gram(step, acc):
                acc = list(acc)
                for u in range(8):
                    t = step * 8 + u
                    x = res[:, lane_tile(t)]
                    y = x * w[pl.ds(t, 1), :]
                    for r in range(shifts):
                        acc[r] = acc[r] + y * (pltpu.roll(x, r, 0) if r else x)
                return tuple(acc)

            acc = lax.fori_loop(0, tiles // 8, gram, tuple(jnp.zeros((SUBS, LANES), F32) for _ in range(shifts)))
            packed = jnp.zeros((SUBS, LANES), F32)
            for r in range(shifts):
                packed = jnp.where(lane == hist_len * r + sub, jnp.sum(acc[r], axis=1, keepdims=True), packed)
            row_buf[pl.ds(me, 1)] = (jnp.sum(packed, axis=0, keepdims=True) + slot_row)[None]
            pl.semaphore_wait(barrier, devices - 1)
        else:
            slot = slot_index[iteration - 1]
            replaced = sub == slot

            def refresh(step, acc):
                for u in range(8):
                    t = step * 8 + u
                    new_res = jnp.where(replaced, fresh[pl.ds(t, 1), :], res[:, lane_tile(t)])
                    new_rho = jnp.where(replaced, density_out[pl.ds(t, 1), :], rho[:, lane_tile(t)])
                    res[:, lane_tile(t)] = new_res
                    rho[:, lane_tile(t)] = new_rho
                    acc = acc + fresh_w[pl.ds(t, 1), :] * new_res
                return acc

            acc = lax.fori_loop(0, tiles // 8, refresh, jnp.zeros((SUBS, LANES), F32))
            packed = jnp.where(lane == sub, jnp.sum(acc, axis=1, keepdims=True), 0.0)
            row_buf[pl.ds(me, 1)] = jnp.sum(packed, axis=0, keepdims=True)[None]
        wait = exchange(row_buf, 2 * iteration)

        if iteration == 0:
            loads[2].wait()

        @pl.loop(0, rows)
        def _(r):
            xs, ys = [], []
            for q in range(4):
                b = q * rows + r
                at = pl.ds(pl.multiple_of(b * width, width), width)
                gain = jnp.concatenate([w[pl.ds(b * per_batch + v, 1), :] for v in range(per_batch)], axis=1)
                xs.extend(split(res[:, at] * gain))
                ys.append(jnp.concatenate([basis[0:24, at], jnp.broadcast_to(basis[24:25, at], (SUBS, width))], axis=0))
            x = jnp.concatenate(xs, axis=0).astype(jnp.bfloat16)
            out = None
            for y in split(jnp.concatenate(ys, axis=0)):
                part = lax.dot_general(
                    x, y.astype(jnp.bfloat16), (((1,), (1,)), ((), ())), preferred_element_type=F32
                )
                out = part if out is None else out + part
            tile = jnp.zeros((SUBS, LANES), F32)
            for q in range(4):
                block = out[24 * q : 24 * q + 8] + out[24 * q + 8 : 24 * q + 16] + out[24 * q + 16 : 24 * q + 24]
                tile = jnp.where(quarter == q, block, tile)
            hist_moments[r] = tile

        wait()

        row = total_row(row_buf)
        if iteration == 0:
            entry = [[None] * (i + 1) for i in range(hist_len)]
            for i in range(hist_len):
                for j in range(i + 1):
                    r = i - j
                    at = hist_len * r + i if r < shifts else hist_len * (hist_len - r) + j
                    entry[i][j] = splat(row, at)
        else:
            news = [splat(row, k) for k in range(hist_len)]
            slot_vec = jnp.zeros((1, LANES), jnp.int32) + slot
            entry = [
                [
                    jnp.where(slot_vec == i, news[j], jnp.where(slot_vec == j, news[i], entry[i][j]))
                    for j in range(i + 1)
                ]
                for i in range(hist_len)
            ]
        coeffs = solve_coeffs(entry, hist_len)
        coeff_col = jnp.zeros((SUBS, LANES), F32)
        for i in range(hist_len):
            coeff_col = jnp.where(sub == i, coeffs[i], coeff_col)

        mixed = [jnp.sum(coeff_col * hist_moments[r], axis=0, keepdims=True) for r in range(rows)]
        moment_buf[pl.ds(me, 1)] = jnp.concatenate(mixed, axis=0)[None]
        wait = exchange(moment_buf, 2 * iteration + 1)

        if iteration == 0:
            base = (my_member * owned).astype(F32)
            wide = lax.broadcasted_iota(jnp.int32, (owned, LANES), 0).astype(F32) + base

            @pl.loop(0, devices // SUBS)
            def _(c):
                ids = jnp.concatenate([row_buf[c * SUBS + i] for i in range(SUBS)], axis=0)
                stepped = pltpu.roll(ids, 0, 1, stride=rows, stride_axis=0)
                for q in range(4):
                    turned = pltpu.roll(stepped, (half - rows * q) % LANES, 1)
                    slots = jnp.sum(jnp.where(lane // rows == sub, turned, 0.0), axis=0, keepdims=True)
                    near[q * batches : (q + 1) * batches, lane_tile(c)] = jnp.where(
                        slot_col == slots, 1.0, 0.0
                    ).astype(jnp.bfloat16)
                    own[q * owned : (q + 1) * owned, lane_tile(c)] = jnp.where(wide == slots, 1.0, 0.0).astype(
                        jnp.bfloat16
                    )

            for load in loads[3:]:
                load.wait()

        def base_step(step, carry):
            for u in range(8):
                t = step * 8 + u
                part = coeff_col * (rho[:, lane_tile(t)] + mixing_beta * res[:, lane_tile(t)])
                base_rows[pl.ds(t, 1), :] = jnp.sum(part, axis=0, keepdims=True)
            return carry

        lax.fori_loop(0, tiles // 8, base_step, 0)
        wait()

        everywhere = moment_buf[...].reshape(devices * rows, LANES)
        pieces = jnp.concatenate([piece.astype(jnp.bfloat16) for piece in split(everywhere)], axis=1)

        def gathered(mask, count):
            out = jnp.dot(mask[...], pieces, preferred_element_type=F32)
            out = out[:, 0:LANES] + out[:, LANES : 2 * LANES] + out[:, 2 * LANES :]
            group = lax.broadcasted_iota(jnp.int32, (count, LANES), 1) // 32
            total = out[0:count]
            for q in range(1, 4):
                total = jnp.where(group == q, out[q * count : (q + 1) * count], total)
            total = total + pltpu.roll(total, 64, 1)
            total = total + pltpu.roll(total, 32, 1)
            return jnp.transpose(jnp.concatenate([total] * max(1, LANES // count), axis=0))[0:32] * scale

        at_batch = gathered(near, batches)
        comp = lax.broadcasted_iota(jnp.int32, (32, LANES), 0)
        degree = sum((comp >= (l + 1) * (l + 1)).astype(F32) for l in range(4))
        damped = jnp.where(comp < harmonics, at_batch * (mixing_beta / (1.0 + degree)), 0.0)

        def density_step(step, ahead):
            for u in range(16):
                b = step * 16 + u
                col = jnp.broadcast_to(ahead[:, u : u + 1], (32, LANES))
                for v in range(per_batch):
                    t = b * per_batch + v
                    part = col[24:32] * basis[24:25, lane_tile(t)]
                    for g in range(3):
                        part = part + col[g * SUBS : (g + 1) * SUBS] * basis[g * SUBS : (g + 1) * SUBS, lane_tile(t)]
                    correct[pl.ds(t, 1), :] = jnp.sum(part, axis=0, keepdims=True)
            return pltpu.roll(ahead, LANES - 16, 1)

        lax.fori_loop(0, batches // 16, density_step, damped)
        density = base_rows[...] - correct[...]
        density_out[...] = density
        if last:
            moments_out[...] = gathered(own, owned)[0:harmonics]
        else:
            new = target[...] + coupling[...] * jnp.tanh(density) - density
            fresh[...] = new
            fresh_w[...] = new * w[...]


def finish(density, moments, density_out, moments_out):
    density_out[...] = density[...]
    moments_out[...] = moments[...]


def local(weights, target, coupling, multipole_basis, rho_hist, res_hist, batch_atom, owner_slot, slot_index):
    harmonics, points = multipole_basis.shape
    hist_len = res_hist.shape[0]
    batches = batch_atom.shape[0]
    groups = lax.axis_size("grid")
    members = lax.axis_size("atom")
    devices = groups * members
    owned = owner_slot.shape[0] // members
    scale = 1.0 / math.sqrt(points * groups // owned)
    iters = slot_index.shape[0]
    cfg = (iters, hist_len, harmonics, batches, points // batches, owned, groups, members, scale)
    tiles = points // LANES
    flat = (tiles, LANES)
    any_space = pl.BlockSpec(memory_space=pl.ANY)
    smem = pl.BlockSpec(memory_space=pltpu.SMEM)
    vmem = pl.BlockSpec(memory_space=pltpu.VMEM)
    density, moments = pl.pallas_call(
        functools.partial(kernel, cfg),
        out_shape=(jax.ShapeDtypeStruct(flat, F32), jax.ShapeDtypeStruct((harmonics, owned), F32)),
        in_specs=[smem] * 3 + [any_space] * 6,
        out_specs=(vmem, vmem),
        scratch_shapes=[
            pltpu.VMEM(flat, F32),
            pltpu.VMEM(flat, F32),
            pltpu.VMEM(flat, F32),
            pltpu.VMEM((harmonics, points), F32),
            pltpu.VMEM((hist_len, points), F32),
            pltpu.VMEM((hist_len, points), F32),
            pltpu.VMEM(flat, F32),
            pltpu.VMEM(flat, F32),
            pltpu.VMEM((iters, devices, 1, LANES), F32),
            pltpu.VMEM((iters, devices, batches // 4, LANES), F32),
            pltpu.VMEM((4 * batches, devices * batches // 4), jnp.bfloat16),
            pltpu.VMEM((4 * owned, devices * batches // 4), jnp.bfloat16),
            pltpu.VMEM((batches // 4, SUBS, LANES), F32),
            pltpu.VMEM(flat, F32),
            pltpu.VMEM(flat, F32),
            pltpu.SemaphoreType.DMA((6,)),
            pltpu.SemaphoreType.DMA((2 * iters, devices)),
            pltpu.SemaphoreType.DMA((2 * iters, devices)),
        ],
        compiler_params=pltpu.CompilerParams(
            collective_id=0, has_side_effects=True, vmem_limit_bytes=67043328
        ),
    )(
        batch_atom,
        owner_slot,
        slot_index,
        weights.reshape(flat),
        target.reshape(flat),
        coupling.reshape(flat),
        multipole_basis,
        rho_hist,
        res_hist,
    )
    density, moments = pl.pallas_call(
        finish,
        out_shape=(jax.ShapeDtypeStruct(flat, F32), jax.ShapeDtypeStruct((harmonics, owned), F32)),
        in_specs=[vmem] * 2,
        out_specs=(vmem, vmem),
    )(density, moments)
    return density.reshape(points), moments


def solution(mesh):
    both = ("grid", "atom")
    placed = (P(both), P(both), P(both), P(None, both), P(None, both), P(None, both), P(both), P(), P())
    return jax.shard_map(
        local,
        mesh=mesh,
        in_specs=placed,
        out_specs=(P(both), P(None, "atom")),
        check_vma=False,
    )
```

profile of v0, /device:TPU:2, one launch (start us, length us, event | category | flops | bytes accessed | tf_op | source)
XLA Modules:
  0.0 177.3 jit_solution(18058854417176453914)
XLA Ops:
  0.6 175.1 %shard_map.104 = (f32[128,128]{1,0:T(8,128)}, f32[25,512]{1,0:T(8,128)}) custom-call(s32[64]{0:T(128)} %batch_atom.1, s32[4096]{0:T(1024)} %owner_slot.1, s32[2]{0:T(128)} %slot_index.1, f32[128,128]{1,0:T(8,128)} %bitcast.4, f32[128,128]{1,0:T(8,128)} %bitcast.5, f32[128,128]{1,0:T(8,128)} %bitcast.6, f32[25,16384]{1,0:T(8,128)} %basis_hbm.1, ...), custom_call_target="tpu_custom_call" | custom-call | tf_op jit(solution)/shard_map/pallas_call | solution.py:368
  175.8 1.5 shard_map.105
where the time goes:
time: 181 us; the launch traced here: 177 us
  Pallas kernels  177 us (98%)
    pallas_call x1, Pallas kernels, local(): pl.pallas_call(functools.partial(kernel, cfg), out_shape=(jax.ShapeDtypeS...  175 us

commit v1 on v0

v1 whole, which is shorter than its diff:
```python
import functools
import math

import jax
import jax.numpy as jnp
from jax import lax
from jax.experimental import pallas as pl
from jax.experimental.pallas import tpu as pltpu
from jax.sharding import PartitionSpec as P

MESH = pl.DeviceIdType.MESH
LANES = 128
SUBS = 8
mixing_beta = 0.5
ridge_share = 0.1
F32 = jnp.float32


def solve_coeffs(entry, hist_len):
    trace = entry[0][0]
    for i in range(1, hist_len):
        trace = trace + entry[i][i]
    ridge = (ridge_share / hist_len) * trace
    low = [[entry[i][j] for j in range(i + 1)] for i in range(hist_len)]
    for i in range(hist_len):
        low[i][i] = low[i][i] + ridge
    inverse = [None] * hist_len
    factor = [[None] * hist_len for _ in range(hist_len)]
    forward = [jnp.ones_like(trace) for _ in range(hist_len)]
    for j in range(hist_len):
        inverse[j] = 1.0 / low[j][j]
        for i in range(j + 1, hist_len):
            factor[i][j] = low[i][j] * inverse[j]
        for i in range(j + 1, hist_len):
            forward[i] = forward[i] - factor[i][j] * forward[j]
            for k in range(j + 1, i + 1):
                low[i][k] = low[i][k] - factor[i][j] * low[k][j]
    backward = [forward[i] * inverse[i] for i in range(hist_len)]
    for j in reversed(range(hist_len)):
        for i in range(j):
            backward[i] = backward[i] - factor[j][i] * backward[j]
    total = backward[0]
    for i in range(1, hist_len):
        total = total + backward[i]
    return [backward[i] / total for i in range(hist_len)]


def split(x):
    pieces = []
    for _ in range(3):
        piece = x.astype(jnp.bfloat16).astype(F32)
        pieces.append(piece)
        x = x - piece
    return pieces


def kernel(
    cfg,
    batch_atom,
    owner_slot,
    slot_index,
    w_hbm,
    target_hbm,
    coupling_hbm,
    basis_hbm,
    rho_hbm,
    res_hbm,
    density_out,
    moments_out,
    w,
    target,
    coupling,
    basis,
    rho,
    res,
    fresh,
    fresh_w,
    stack_rows,
    plane_rows,
    stack_moments,
    part_send,
    part_recv,
    own_send,
    own_recv,
    chunks,
    source_cols,
    mask,
    hist_moments,
    base_rows,
    correct,
    load_sem,
    send_sem,
    recv_sem,
):
    iters, hist_len, harmonics, batches, width, owned, planes, lines, members, scale = cfg
    tiles = w.shape[0]
    per_batch = width // LANES
    half = LANES // 2
    rows = batches // 4
    plane = lines * members
    near_lanes = plane * batches
    shares = chunks.shape[0]
    depth = shares // lines
    share = owned // shares
    my_group = lax.axis_index("grid")
    my_member = lax.axis_index("atom")
    my_plane = lax.div(my_group, lines)
    my_line = lax.rem(my_group, lines)
    spot = my_line * members + my_member
    my_share = my_line * depth + lax.rem(my_plane, depth)

    def in_stack(at):
        return at * lines + my_line, my_member

    def in_plane(at):
        return my_plane * lines + lax.div(at, members), lax.rem(at, members)

    def in_shares(at):
        return (lax.div(my_plane, depth) * depth + lax.rem(at, depth)) * lines + lax.div(at, depth), my_member

    groups = ((planes, my_plane, in_stack), (plane, spot, in_plane), (shares, my_share, in_shares))
    barrier = pltpu.get_barrier_semaphore()
    for count, mine, where in groups:

        @pl.loop(1, count)
        def _(step):
            pl.semaphore_signal(barrier, inc=1, device_id=where(lax.rem(mine + step, count)), device_id_type=MESH)

    loads = [
        pltpu.make_async_copy(src, dst, load_sem.at[k])
        for k, (src, dst) in enumerate(
            ((res_hbm, res), (w_hbm, w), (basis_hbm, basis), (rho_hbm, rho), (target_hbm, target), (coupling_hbm, coupling))
        )
    ]
    for load in loads:
        load.start()

    lane = lax.broadcasted_iota(jnp.int32, (SUBS, LANES), 1)
    sub = lax.broadcasted_iota(jnp.int32, (SUBS, LANES), 0)
    quarter = lane // 32
    lane_row = lax.broadcasted_iota(jnp.int32, (1, LANES), 1)
    low_row = lane_row < half
    low = lax.broadcasted_iota(jnp.int32, (2 * SUBS, LANES), 1) < half

    slot_row = jnp.zeros((1, LANES), F32)
    for b in range(batches):
        slot_row = jnp.where(lane_row == half + b, owner_slot[batch_atom[b]].astype(F32), slot_row)

    def lane_tile(t):
        return pl.ds(pl.multiple_of(t * LANES, LANES), LANES)

    def copy_to(src, dst, which, group, target_at, source_at):
        return pltpu.make_async_remote_copy(
            src_ref=src,
            dst_ref=dst,
            send_sem=send_sem.at[which, target_at],
            recv_sem=recv_sem.at[which, source_at],
            device_id=groups[group][2](target_at),
            device_id_type=MESH,
        )

    def exchange(buf, which, group):
        count, mine, _ = groups[group]

        @pl.loop(1, count)
        def _(step):
            copy_to(buf.at[mine], buf.at[mine], which, group, lax.rem(mine + step, count), mine).start()

        return waiter(buf, buf, which, group)

    def waiter(src, dst, which, group):
        count, mine, _ = groups[group]

        def wait():
            @pl.loop(1, count)
            def _(step):
                at = lax.rem(mine + step, count)
                copy_to(src.at[at], dst.at[at], which, group, at, at).wait_recv()

            @pl.loop(1, count)
            def _(step):
                at = lax.rem(mine + step, count)
                copy_to(src.at[at], dst.at[at], which, group, at, at).wait_send()

        return wait

    def tree(parts):
        parts = list(parts)
        while len(parts) > 1:
            parts = [parts[k] + parts[k + 1] if k + 1 < len(parts) else parts[k] for k in range(0, len(parts), 2)]
        return parts[0]

    def total(buf, count):
        return tree(buf[k] for k in range(count))

    def splat(row, k):
        return jnp.broadcast_to(row[:, k : k + 1], (1, LANES))

    def weigh(first, last):
        @pl.loop(first, last)
        def _(r):
            xs, ys = [], []
            for q in range(4):
                b = q * rows + r
                at = pl.ds(pl.multiple_of(b * width, width), width)
                gain = jnp.concatenate([w[pl.ds(b * per_batch + v, 1), :] for v in range(per_batch)], axis=1)
                xs.extend(split(res[:, at] * gain))
                ys.append(jnp.concatenate([basis[0:24, at], jnp.broadcast_to(basis[24:25, at], (SUBS, width))], axis=0))
            x = jnp.concatenate(xs, axis=0).astype(jnp.bfloat16)
            out = None
            for y in split(jnp.concatenate(ys, axis=0)):
                part = lax.dot_general(
                    x, y.astype(jnp.bfloat16), (((1,), (1,)), ((), ())), preferred_element_type=F32
                )
                out = part if out is None else out + part
            tile = jnp.zeros((SUBS, LANES), F32)
            for q in range(4):
                block = out[24 * q : 24 * q + 8] + out[24 * q + 8 : 24 * q + 16] + out[24 * q + 16 : 24 * q + 24]
                tile = jnp.where(quarter == q, block, tile)
            hist_moments[r] = tile

    shifts = hist_len // 2 + 1
    entry = None
    per_iter = 4
    for iteration in range(iters):
        stack_row = stack_rows.at[iteration]
        plane_row = plane_rows.at[iteration]
        stack_moment = stack_moments.at[iteration]
        sent = part_send.at[iteration]
        received = part_recv.at[iteration]
        which = per_iter * iteration
        last = iteration == iters - 1

        if iteration == 0:
            loads[0].wait()
            loads[1].wait()

            def gram(step, acc):
                acc = list(acc)
                for u in range(8):
                    t = step * 8 + u
                    x = res[:, lane_tile(t)]
                    y = x * w[pl.ds(t, 1), :]
                    for r in range(shifts):
                        acc[r] = acc[r] + y * (pltpu.roll(x, r, 0) if r else x)
                return tuple(acc)

            acc = lax.fori_loop(0, tiles // 8, gram, tuple(jnp.zeros((SUBS, LANES), F32) for _ in range(shifts)))
            packed = jnp.zeros((SUBS, LANES), F32)
            for r in range(shifts):
                packed = jnp.where(lane == hist_len * r + sub, jnp.sum(acc[r], axis=1, keepdims=True), packed)
            stack_row[pl.ds(my_plane, 1)] = (jnp.sum(packed, axis=0, keepdims=True) + slot_row)[None]
            pl.semaphore_wait(barrier, sum(count - 1 for count, _, _ in groups))
        else:
            slot = slot_index[iteration - 1]
            replaced = sub == slot

            def refresh(step, acc):
                for u in range(8):
                    t = step * 8 + u
                    new_res = jnp.where(replaced, fresh[pl.ds(t, 1), :], res[:, lane_tile(t)])
                    new_rho = jnp.where(replaced, density_out[pl.ds(t, 1), :], rho[:, lane_tile(t)])
                    res[:, lane_tile(t)] = new_res
                    rho[:, lane_tile(t)] = new_rho
                    acc = acc + fresh_w[pl.ds(t, 1), :] * new_res
                return acc

            acc = lax.fori_loop(0, tiles // 8, refresh, jnp.zeros((SUBS, LANES), F32))
            packed = jnp.where(lane == sub, jnp.sum(acc, axis=1, keepdims=True), 0.0)
            stack_row[pl.ds(my_plane, 1)] = jnp.sum(packed, axis=0, keepdims=True)[None]
        wait = exchange(stack_row, which, 0)

        if iteration == 0:
            loads[2].wait()
        weigh(0, rows // 2)

        wait()
        plane_row[pl.ds(spot, 1)] = jnp.where(low_row, total(stack_row, planes), slot_row)[None]
        wait = exchange(plane_row, which + 1, 1)

        if iteration == 0:
            ids = jnp.concatenate([stack_row[k] for k in range(planes)] * (LANES // planes), axis=0)
            ids = jnp.transpose(ids)
            for k in range(planes):
                source_cols[k * batches : (k + 1) * batches] = jnp.broadcast_to(
                    ids[half : half + batches, k : k + 1], (batches, LANES)
                )
        weigh(rows // 2, rows)

        wait()
        row = total(plane_row, plane)
        if iteration == 0:
            entry = [[None] * (i + 1) for i in range(hist_len)]
            for i in range(hist_len):
                for j in range(i + 1):
                    r = i - j
                    at = hist_len * r + i if r < shifts else hist_len * (hist_len - r) + j
                    entry[i][j] = splat(row, at)
        else:
            news = [splat(row, k) for k in range(hist_len)]
            slot_vec = jnp.zeros((1, LANES), jnp.int32) + slot
            entry = [
                [
                    jnp.where(slot_vec == i, news[j], jnp.where(slot_vec == j, news[i], entry[i][j]))
                    for j in range(i + 1)
                ]
                for i in range(hist_len)
            ]
        coeffs = solve_coeffs(entry, hist_len)
        coeff_col = jnp.zeros((SUBS, LANES), F32)
        for i in range(hist_len):
            coeff_col = jnp.where(sub == i, coeffs[i], coeff_col)

        mixed = jnp.concatenate(
            [jnp.sum(coeff_col * hist_moments[r], axis=0, keepdims=True) for r in range(rows)], axis=0
        )
        turned = jnp.concatenate(
            [
                pltpu.roll(mixed, (LANES - 32 * q - 16 * h) % LANES, 1) if q + h else mixed
                for h in range(2)
                for q in range(4)
            ],
            axis=0,
        )
        stack_moment[pl.ds(my_plane, 1)] = jnp.transpose(turned)[0 : 2 * SUBS][None]
        wait = exchange(stack_moment, which + 2, 0)

        if iteration == 0:

            def fill(lanes, wanted):
                for k in range(mask.shape[0] // (2 * SUBS)):
                    at = slice(2 * SUBS * k, 2 * SUBS * (k + 1))
                    mask[at, lanes] = jnp.where(source_cols[at] == wanted, 1.0, 0.0).astype(jnp.bfloat16)

            @pl.loop(0, near_lanes // LANES)
            def _(t):
                pair = jnp.where(low_row, pltpu.roll(plane_row[2 * t], half, 1), plane_row[2 * t + 1])
                fill(lane_tile(t), pair)

            @pl.loop(0, plane * share // LANES)
            def _(t):
                at = t * (LANES // share) + lane_row // share
                held = (at % members) * owned + ((at // members) * depth + lax.rem(my_plane, depth)) * share
                fill(lane_tile(t + near_lanes // LANES), (held + lane_row % share).astype(F32))

            for load in loads[3:]:
                load.wait()

        def base_step(step, carry):
            for u in range(8):
                t = step * 8 + u
                part = coeff_col * (rho[:, lane_tile(t)] + mixing_beta * res[:, lane_tile(t)])
                base_rows[pl.ds(t, 1), :] = jnp.sum(part, axis=0, keepdims=True)
            return carry

        lax.fori_loop(0, tiles // 8, base_step, 0)
        wait()

        blocks = []
        for k in range(0, planes, 2):
            one, two = stack_moment[k], stack_moment[k + 1]
            upper = jnp.where(low, one, pltpu.roll(two, half, 1))
            lower = jnp.where(low, pltpu.roll(one, half, 1), two)
            blocks.append(jnp.concatenate([upper, lower], axis=0))
        everywhere = jnp.concatenate(blocks, axis=1)
        pieces = jnp.concatenate(split(everywhere), axis=0).astype(jnp.bfloat16)

        def gathered(first, count):
            out = jnp.dot(
                pieces, mask[:, pl.ds(pl.multiple_of(first, count), count)], preferred_element_type=F32
            )
            return out[0:32] + out[32:64] + out[64:96]

        quad = 4

        @pl.loop(0, plane // quad)
        def _(step):
            first = lax.rem(lax.div(spot, quad) + step, plane // quad) * quad
            out = gathered(first * batches, quad * batches)
            for k in range(0, quad, 2):
                upper = out[0:16, k * batches : (k + 2) * batches]
                lower = out[16:32, k * batches : (k + 2) * batches]
                sent[first + k] = jnp.where(low, upper, pltpu.roll(lower, half, 1))
                sent[first + k + 1] = jnp.where(low, pltpu.roll(upper, half, 1), lower)
            for k in range(quad):

                @pl.when(first + k != spot)
                def _():
                    copy_to(sent.at[first + k], received.at[spot], which + 3, 1, first + k, spot).start()

        received[pl.ds(spot, 1)] = sent[pl.ds(spot, 1)]
        wait = waiter(sent, received, which + 3, 1)

        if last:
            many = 2 * LANES // share
            each = LANES // share

            @pl.loop(0, plane // many)
            def _(step):
                first = lax.rem(lax.div(spot, many) + step, plane // many) * many
                out = gathered(near_lanes + first * share, many * share)
                for k in range(many):
                    tile = out[:, k // each * LANES : (k // each + 1) * LANES]
                    kept = jnp.zeros((SUBS, LANES), F32)
                    for g in range(4):
                        piece = tile[g * SUBS : (g + 1) * SUBS]
                        turn = (g - k % each) * 32 % LANES
                        kept = jnp.where(quarter == g, pltpu.roll(piece, turn, 1) if turn else piece, kept)
                    own_send[first + k] = kept
                for k in range(many):

                    @pl.when(first + k != spot)
                    def _():
                        copy_to(own_send.at[first + k], own_recv.at[spot], per_iter * iters, 1, first + k, spot).start()

            own_recv[pl.ds(spot, 1)] = own_send[pl.ds(spot, 1)]
            own_wait = waiter(own_send, own_recv, per_iter * iters, 1)

        wait()
        summed = total(received, plane)
        at_batch = jnp.concatenate([summed, pltpu.roll(summed, half, 1)], axis=0) * scale
        if last:
            own_wait()
            chunks[pl.ds(my_share, 1)] = (total(own_recv, plane) * scale)[None]
            own_wait = exchange(chunks, per_iter * iters + 1, 2)

        comp = lax.broadcasted_iota(jnp.int32, (32, LANES), 0)
        degree = sum((comp >= (l + 1) * (l + 1)).astype(F32) for l in range(4))
        damped = jnp.where(comp < harmonics, at_batch * (mixing_beta / (1.0 + degree)), 0.0)

        def density_step(step, ahead):
            for u in range(16):
                b = step * 16 + u
                col = jnp.broadcast_to(ahead[:, u : u + 1], (32, LANES))
                for v in range(per_batch):
                    t = b * per_batch + v
                    part = col[24:32] * basis[24:25, lane_tile(t)]
                    for g in range(3):
                        part = part + col[g * SUBS : (g + 1) * SUBS] * basis[g * SUBS : (g + 1) * SUBS, lane_tile(t)]
                    correct[pl.ds(t, 1), :] = jnp.sum(part, axis=0, keepdims=True)
            return pltpu.roll(ahead, LANES - 16, 1)

        lax.fori_loop(0, batches // 16, density_step, damped)
        density = base_rows[...] - correct[...]
        density_out[...] = density
        if last:
            own_wait()
            each = LANES // share
            for t in range(owned // LANES):
                held = [chunks[t * each + k] for k in range(each)]
                for g in range(4):
                    tile = jnp.zeros((SUBS, LANES), F32)
                    for k in range(each):
                        turn = (k - g) * 32 % LANES
                        tile = jnp.where(quarter == k, pltpu.roll(held[k], turn, 1) if turn else held[k], tile)
                    top = min(SUBS, harmonics - g * SUBS)
                    moments_out[g * SUBS : g * SUBS + top, t * LANES : (t + 1) * LANES] = tile[0:top]
        else:
            new = target[...] + coupling[...] * jnp.tanh(density) - density
            fresh[...] = new
            fresh_w[...] = new * w[...]


def finish(density, moments, density_out, moments_out):
    density_out[...] = density[...]
    moments_out[...] = moments[...]


def local(weights, target, coupling, multipole_basis, rho_hist, res_hist, batch_atom, owner_slot, slot_index):
    harmonics, points = multipole_basis.shape
    hist_len = res_hist.shape[0]
    batches = batch_atom.shape[0]
    groups = lax.axis_size("grid")
    members = lax.axis_size("atom")
    lines = 4
    planes = groups // lines
    plane = lines * members
    shares = 4 * lines
    owned = owner_slot.shape[0] // members
    scale = 1.0 / math.sqrt(points * groups // owned)
    iters = slot_index.shape[0]
    cfg = (iters, hist_len, harmonics, batches, points // batches, owned, planes, lines, members, scale)
    tiles = points // LANES
    flat = (tiles, LANES)
    any_space = pl.BlockSpec(memory_space=pl.ANY)
    smem = pl.BlockSpec(memory_space=pltpu.SMEM)
    vmem = pl.BlockSpec(memory_space=pltpu.VMEM)
    density, moments = pl.pallas_call(
        functools.partial(kernel, cfg),
        out_shape=(jax.ShapeDtypeStruct(flat, F32), jax.ShapeDtypeStruct((harmonics, owned), F32)),
        in_specs=[smem] * 3 + [any_space] * 6,
        out_specs=(vmem, vmem),
        scratch_shapes=[
            pltpu.VMEM(flat, F32),
            pltpu.VMEM(flat, F32),
            pltpu.VMEM(flat, F32),
            pltpu.VMEM((harmonics, points), F32),
            pltpu.VMEM((hist_len, points), F32),
            pltpu.VMEM((hist_len, points), F32),
            pltpu.VMEM(flat, F32),
            pltpu.VMEM(flat, F32),
            pltpu.VMEM((iters, planes, 1, LANES), F32),
            pltpu.VMEM((iters, plane, 1, LANES), F32),
            pltpu.VMEM((iters, planes, 2 * SUBS, LANES), F32),
            pltpu.VMEM((iters, plane, 2 * SUBS, LANES), F32),
            pltpu.VMEM((iters, plane, 2 * SUBS, LANES), F32),
            pltpu.VMEM((plane, SUBS, LANES), F32),
            pltpu.VMEM((plane, SUBS, LANES), F32),
            pltpu.VMEM((shares, SUBS, LANES), F32),
            pltpu.VMEM((planes * batches, LANES), F32),
            pltpu.VMEM((planes * batches, plane * (batches + owned // shares)), jnp.bfloat16),
            pltpu.VMEM((batches // 4, SUBS, LANES), F32),
            pltpu.VMEM(flat, F32),
            pltpu.VMEM(flat, F32),
            pltpu.SemaphoreType.DMA((6,)),
            pltpu.SemaphoreType.DMA((4 * iters + 2, plane)),
            pltpu.SemaphoreType.DMA((4 * iters + 2, plane)),
        ],
        compiler_params=pltpu.CompilerParams(
            collective_id=0, has_side_effects=True, vmem_limit_bytes=67043328
        ),
    )(
        batch_atom,
        owner_slot,
        slot_index,
        weights.reshape(flat),
        target.reshape(flat),
        coupling.reshape(flat),
        multipole_basis,
        rho_hist,
        res_hist,
    )
    density, moments = pl.pallas_call(
        finish,
        out_shape=(jax.ShapeDtypeStruct(flat, F32), jax.ShapeDtypeStruct((harmonics, owned), F32)),
        in_specs=[vmem] * 2,
        out_specs=(vmem, vmem),
    )(density, moments)
    return density.reshape(points), moments


def solution(mesh):
    both = ("grid", "atom")
    placed = (P(both), P(both), P(both), P(None, both), P(None, both), P(None, both), P(both), P(), P())
    return jax.shard_map(
        local,
        mesh=mesh,
        in_specs=placed,
        out_specs=(P(both), P(None, "atom")),
        check_vma=False,
    )
```

time: 181 us -> 72.3 us (0.40)
  the two profiles are of different devices: /device:TPU:2 before, /device:TPU:1 now
where the time goes in v1:
time: 72.3 us; the launch traced here: 72.1 us
  Pallas kernels  71.5 us (99%)
    pallas_call x1, Pallas kernels, local(): pl.pallas_call(functools.partial(kernel, cfg), out_shape=(jax.ShapeDtypeS...  70 us
    pallas_call x1, Pallas kernels, local(): pl.pallas_call(finish, out_shape=(jax.ShapeDtypeStruct(flat, F32), jax.Sh...  1.53 us

profile of v1, /device:TPU:1, one launch (start us, length us, event | category | flops | bytes accessed | tf_op | source)
XLA Modules:
  0.0 72.1 jit_solution(12247511344697249004)
XLA Ops:
  0.6 70.0 %shard_map.104 = (f32[128,128]{1,0:T(8,128)}, f32[25,512]{1,0:T(8,128)}) custom-call(s32[64]{0:T(128)} %batch_atom.1, s32[4096]{0:T(1024)} %owner_slot.1, s32[2]{0:T(128)} %slot_index.1, f32[128,128]{1,0:T(8,128)} %bitcast.4, f32[128,128]{1,0:T(8,128)} %bitcast.5, f32[128,128]{1,0:T(8,128)} %bitcast.6, f32[25,16384]{1,0:T(8,128)} %basis_hbm.1, ...), custom_call_target="tpu_custom_call" | custom-call | tf_op jit(solution)/shard_map/pallas_call | solution.py:488
  70.6 1.5 %shard_map.105 = (f32[128,128]{1,0:T(8,128)}, f32[25,512]{1,0:T(8,128)}) custom-call(f32[128,128]{1,0:T(8,128)} %get-tuple-element.6.density, f32[25,512]{1,0:T(8,128)} %get-tuple-element.7.moments), custom_call_target="tpu_custom_call" | custom-call | tf_op jit(solution)/shard_map/pallas_call | solution.py:533

commit v2 on v1

--- a/solution.py
+++ b/solution.py
@@ -149,12 +149,12 @@
     def lane_tile(t):
         return pl.ds(pl.multiple_of(t * LANES, LANES), LANES)
 
-    def copy_to(src, dst, which, group, target_at, source_at):
+    def copy_to(src, dst, which, group, target_at):
         return pltpu.make_async_remote_copy(
             src_ref=src,
             dst_ref=dst,
-            send_sem=send_sem.at[which, target_at],
-            recv_sem=recv_sem.at[which, source_at],
+            send_sem=send_sem.at[which],
+            recv_sem=recv_sem.at[which],
             device_id=groups[group][2](target_at),
             device_id_type=MESH,
         )
@@ -164,23 +164,19 @@
 
         @pl.loop(1, count)
         def _(step):
-            copy_to(buf.at[mine], buf.at[mine], which, group, lax.rem(mine + step, count), mine).start()
+            copy_to(buf.at[mine], buf.at[mine], which, group, lax.rem(mine + step, count)).start()
 
         return waiter(buf, buf, which, group)
 
+    sends = []
+
     def waiter(src, dst, which, group):
-        count, mine, _ = groups[group]
+        all_but_one = pl.ds(0, groups[group][0] - 1)
+        sends.append((src.at[all_but_one], send_sem.at[which]))
 
         def wait():
-            @pl.loop(1, count)
-            def _(step):
-                at = lax.rem(mine + step, count)
-                copy_to(src.at[at], dst.at[at], which, group, at, at).wait_recv()
-
-            @pl.loop(1, count)
-            def _(step):
-                at = lax.rem(mine + step, count)
-                copy_to(src.at[at], dst.at[at], which, group, at, at).wait_send()
+            arrived = dst.at[all_but_one]
+            pltpu.make_async_copy(arrived, arrived, recv_sem.at[which]).wait()
 
         return wait
 
@@ -386,7 +382,7 @@
 
                 @pl.when(first + k != spot)
                 def _():
-                    copy_to(sent.at[first + k], received.at[spot], which + 3, 1, first + k, spot).start()
+                    copy_to(sent.at[first + k], received.at[spot], which + 3, 1, first + k).start()
 
         received[pl.ds(spot, 1)] = sent[pl.ds(spot, 1)]
         wait = waiter(sent, received, which + 3, 1)
@@ -411,7 +407,7 @@
 
                     @pl.when(first + k != spot)
                     def _():
-                        copy_to(own_send.at[first + k], own_recv.at[spot], per_iter * iters, 1, first + k, spot).start()
+                        copy_to(own_send.at[first + k], own_recv.at[spot], per_iter * iters, 1, first + k).start()
 
             own_recv[pl.ds(spot, 1)] = own_send[pl.ds(spot, 1)]
             own_wait = waiter(own_send, own_recv, per_iter * iters, 1)
@@ -459,6 +455,9 @@
             new = target[...] + coupling[...] * jnp.tanh(density) - density
             fresh[...] = new
             fresh_w[...] = new * w[...]
+
+    for src, sem in sends:
+        pltpu.make_async_copy(src, src, sem).wait()
 
 
 def finish(density, moments, density_out, moments_out):
@@ -513,8 +512,8 @@
             pltpu.VMEM(flat, F32),
             pltpu.VMEM(flat, F32),
             pltpu.SemaphoreType.DMA((6,)),
-            pltpu.SemaphoreType.DMA((4 * iters + 2, plane)),
-            pltpu.SemaphoreType.DMA((4 * iters + 2, plane)),
+            pltpu.SemaphoreType.DMA((4 * iters + 2,)),
+            pltpu.SemaphoreType.DMA((4 * iters + 2,)),
         ],
         compiler_params=pltpu.CompilerParams(
             collective_id=0, has_side_effects=True, vmem_limit_bytes=67043328

time: 72.3 us -> 63.5 us (0.88)
  Pallas kernels: 71.5 us -> 62.7 us
    pallas_call x1, Pallas kernels: 70 us -> 61.2 us  [local(): pl.pallas_call(functools.partial(kernel, cfg), out_shape=(jax.ShapeDtypeS...]
where the time goes in v2:
time: 63.5 us; the launch traced here: 63.3 us
  Pallas kernels  62.7 us (99%)
  between operations  0.64 us (1%)
    pallas_call x1, Pallas kernels, local(): pl.pallas_call(functools.partial(kernel, cfg), out_shape=(jax.ShapeDtypeS...  61.2 us
    pallas_call x1, Pallas kernels, local(): pl.pallas_call(finish, out_shape=(jax.ShapeDtypeStruct(flat, F32), jax.Sh...  1.53 us

profile of v2, /device:TPU:1, one launch (start us, length us, event | category | flops | bytes accessed | tf_op | source)
XLA Modules:
  0.0 63.3 jit_solution(8098720569047785709)
XLA Ops:
  0.6 61.2 %shard_map.104 = (f32[128,128]{1,0:T(8,128)}, f32[25,512]{1,0:T(8,128)}) custom-call(s32[64]{0:T(128)} %batch_atom.1, s32[4096]{0:T(1024)} %owner_slot.1, s32[2]{0:T(128)} %slot_index.1, f32[128,128]{1,0:T(8,128)} %bitcast.4, f32[128,128]{1,0:T(8,128)} %bitcast.5, f32[128,128]{1,0:T(8,128)} %bitcast.6, f32[25,16384]{1,0:T(8,128)} %basis_hbm.1, ...), custom_call_target="tpu_custom_call" | custom-call | tf_op jit(solution)/shard_map/pallas_call | solution.py:487
  61.8 1.5 %shard_map.105 = (f32[128,128]{1,0:T(8,128)}, f32[25,512]{1,0:T(8,128)}) custom-call(f32[128,128]{1,0:T(8,128)} %get-tuple-element.6.density, f32[25,512]{1,0:T(8,128)} %get-tuple-element.7.moments), custom_call_target="tpu_custom_call" | custom-call | tf_op jit(solution)/shard_map/pallas_call | solution.py:532

commit v3 on v2

v3 whole, which is shorter than its diff:
```python
import functools
import math

import jax
import jax.numpy as jnp
from jax import lax
from jax.experimental import pallas as pl
from jax.experimental.pallas import tpu as pltpu
from jax.sharding import PartitionSpec as P

MESH = pl.DeviceIdType.MESH
LANES = 128
SUBS = 8
mixing_beta = 0.5
ridge_share = 0.1
F32 = jnp.float32


def solve_coeffs(entry, hist_len):
    trace = entry[0][0]
    for i in range(1, hist_len):
        trace = trace + entry[i][i]
    ridge = (ridge_share / hist_len) * trace
    low = [[entry[i][j] for j in range(i + 1)] for i in range(hist_len)]
    for i in range(hist_len):
        low[i][i] = low[i][i] + ridge
    inverse = [None] * hist_len
    factor = [[None] * hist_len for _ in range(hist_len)]
    forward = [jnp.ones_like(trace) for _ in range(hist_len)]
    for j in range(hist_len):
        inverse[j] = 1.0 / low[j][j]
        for i in range(j + 1, hist_len):
            factor[i][j] = low[i][j] * inverse[j]
        for i in range(j + 1, hist_len):
            forward[i] = forward[i] - factor[i][j] * forward[j]
            for k in range(j + 1, i + 1):
                low[i][k] = low[i][k] - factor[i][j] * low[k][j]
    backward = [forward[i] * inverse[i] for i in range(hist_len)]
    for j in reversed(range(hist_len)):
        for i in range(j):
            backward[i] = backward[i] - factor[j][i] * backward[j]
    total = backward[0]
    for i in range(1, hist_len):
        total = total + backward[i]
    return [backward[i] / total for i in range(hist_len)]


def split(x):
    pieces = []
    for _ in range(3):
        piece = x.astype(jnp.bfloat16).astype(F32)
        pieces.append(piece)
        x = x - piece
    return pieces


def kernel(
    cfg,
    batch_atom,
    owner_slot,
    slot_index,
    w_hbm,
    target_hbm,
    coupling_hbm,
    basis_hbm,
    rho_hbm,
    res_hbm,
    density_out,
    moments_out,
    w,
    target,
    coupling,
    basis,
    rho,
    res,
    fresh,
    fresh_w,
    stack_rows,
    sheet_rows,
    id_rows,
    hist_all,
    fresh_all,
    part_send,
    part_recv,
    own_send,
    own_recv,
    chunks,
    source_cols,
    mask,
    hist_moments,
    base_rows,
    correct,
    load_sem,
    send_sem,
    recv_sem,
    pass_sem,
):
    iters, hist_len, harmonics, batches, width, owned, planes, lines, spans, cores, scale = cfg
    tiles = w.shape[0]
    per_batch = width // LANES
    half = LANES // 2
    rows = batches // 4
    stack = planes * cores
    sheet = lines * spans
    near_lanes = sheet * batches
    shares = chunks.shape[0]
    depth = shares // lines
    share = owned // shares
    my_group = lax.axis_index("grid")
    my_member = lax.axis_index("atom")
    my_plane = lax.div(my_group, lines)
    my_line = lax.rem(my_group, lines)
    my_span = lax.div(my_member, cores)
    my_core = lax.rem(my_member, cores)
    in_stack = my_plane * cores + my_core
    in_sheet = my_line * spans + my_span
    my_share = my_line * depth + lax.rem(my_plane, depth)

    def ring(step, count):
        return min(step, count - step)

    def stack_peer(step):
        plane, core = lax.rem(my_plane + step[0], planes), lax.rem(my_core + step[1], cores)
        return plane * cores + core, (plane * lines + my_line, my_span * cores + core)

    def sheet_peer(step):
        line, span = lax.rem(my_line + step[0], lines), lax.rem(my_span + step[1], spans)
        return line * spans + span, (my_plane * lines + line, span * cores + my_core)

    def share_peer(step):
        line, plane = lax.rem(my_line + step[0], lines), lax.rem(my_plane + step[1], depth)
        device = (lax.div(my_plane, depth) * depth + plane) * lines + line, my_member
        return line * depth + plane, device

    def far_first(across, along):
        steps = [(a, b) for a in range(across) for b in range(along) if a or b]
        return sorted(steps, key=lambda step: -ring(step[0], across) - ring(step[1], along))

    stack_group = (stack, in_stack, stack_peer, far_first(planes, cores))
    sheet_group = (sheet, in_sheet, sheet_peer, far_first(lines, spans))
    share_group = (shares, my_share, share_peer, far_first(lines, depth))
    groups = (stack_group, sheet_group, share_group)
    barrier = pltpu.get_barrier_semaphore()
    for _, _, peer, steps in groups:
        for step in steps:
            pl.semaphore_signal(barrier, inc=1, device_id=peer(step)[1], device_id_type=MESH)

    loads = [
        pltpu.make_async_copy(src, dst, load_sem.at[k])
        for k, (src, dst) in enumerate(
            ((res_hbm, res), (w_hbm, w), (basis_hbm, basis), (rho_hbm, rho), (target_hbm, target), (coupling_hbm, coupling))
        )
    ]
    for load in loads:
        load.start()

    lane = lax.broadcasted_iota(jnp.int32, (SUBS, LANES), 1)
    sub = lax.broadcasted_iota(jnp.int32, (SUBS, LANES), 0)
    quarter = lane // 32
    lane_row = lax.broadcasted_iota(jnp.int32, (1, LANES), 1)
    low_row = lane_row < half
    low = lax.broadcasted_iota(jnp.int32, (2 * SUBS, LANES), 1) < half
    low_wide = lax.broadcasted_iota(jnp.int32, (32, LANES), 1) < half

    slot_row = jnp.zeros((1, LANES), F32)
    for b in range(batches):
        slot_row = jnp.where(lane_row == half + b, owner_slot[batch_atom[b]].astype(F32), slot_row)
    id_rows[pl.ds(in_sheet, 1)] = slot_row[None]

    def lane_tile(t):
        return pl.ds(pl.multiple_of(t * LANES, LANES), LANES)

    kinds = []
    sends = []

    def channel():
        kinds.append(len(kinds))
        return kinds[-1]

    def copy_to(src, dst, which, device, arrival=None):
        return pltpu.make_async_remote_copy(
            src_ref=src,
            dst_ref=dst,
            send_sem=send_sem.at[which],
            recv_sem=recv_sem.at[which] if arrival is None else arrival,
            device_id=device,
            device_id_type=MESH,
        )

    def drained(src, which):
        sends.append((src, send_sem.at[which]))

    def waiter(src, dst, which, count):
        drained(src.at[pl.ds(0, count)], which)

        def wait():
            arrived = dst.at[pl.ds(0, count)]
            pltpu.make_async_copy(arrived, arrived, recv_sem.at[which]).wait()

        return wait

    def exchange(buf, group):
        count, mine, peer, steps = group
        which = channel()
        for step in steps:
            copy_to(buf.at[mine], buf.at[mine], which, peer(step)[1]).start()
        return waiter(buf, buf, which, count - 1)

    def scatter(src, dst, group):
        count, mine, peer, steps = group
        which = channel()

        def send(step):
            at, device = peer(step)
            copy_to(src.at[at], dst.at[mine], which, device).start()

        return send, waiter(src, dst, which, count - 1)

    def tree(parts):
        parts = list(parts)
        while len(parts) > 1:
            parts = [parts[k] + parts[k + 1] if k + 1 < len(parts) else parts[k] for k in range(0, len(parts), 2)]
        return parts[0]

    def total(buf, count):
        return tree(buf[k] for k in range(count))

    def splat(row, k):
        return jnp.broadcast_to(row[:, k : k + 1], (1, LANES))

    def weigh():
        @pl.loop(0, rows // 2)
        def _(step):
            for u in range(2):
                r = step * 2 + u
                xs, ys = [], []
                for q in range(4):
                    b = q * rows + r
                    at = pl.ds(pl.multiple_of(b * width, width), width)
                    gain = jnp.concatenate([w[pl.ds(b * per_batch + v, 1), :] for v in range(per_batch)], axis=1)
                    xs.extend(split(res[:, at] * gain))
                    ys.append(
                        jnp.concatenate([basis[0:24, at], jnp.broadcast_to(basis[24:25, at], (SUBS, width))], axis=0)
                    )
                x = jnp.concatenate(xs, axis=0).astype(jnp.bfloat16)
                out = None
                for y in split(jnp.concatenate(ys, axis=0)):
                    part = lax.dot_general(
                        x, y.astype(jnp.bfloat16), (((1,), (1,)), ((), ())), preferred_element_type=F32
                    )
                    out = part if out is None else out + part
                tile = jnp.zeros((SUBS, LANES), F32)
                for q in range(4):
                    block = out[24 * q : 24 * q + 8] + out[24 * q + 8 : 24 * q + 16] + out[24 * q + 16 : 24 * q + 24]
                    tile = jnp.where(quarter == q, block, tile)
                hist_moments[pl.ds(r, hist_len, stride=rows), :] = tile

    def turn(block, by):
        return pltpu.roll(block, by % LANES, 1) if by % LANES else block

    shifts = hist_len // 2 + 1
    entry = None
    for iteration in range(iters):
        stack_row = stack_rows.at[iteration]
        sheet_row = sheet_rows.at[iteration]
        sent = part_send.at[iteration]
        received = part_recv.at[iteration]
        last = iteration == iters - 1

        if iteration == 0:
            loads[0].wait()
            loads[1].wait()

            def gram(step, acc):
                acc = list(acc)
                for u in range(8):
                    t = step * 8 + u
                    x = res[:, lane_tile(t)]
                    y = x * w[pl.ds(t, 1), :]
                    for r in range(shifts):
                        acc[r] = acc[r] + y * (pltpu.roll(x, r, 0) if r else x)
                return tuple(acc)

            acc = lax.fori_loop(0, tiles // 8, gram, tuple(jnp.zeros((SUBS, LANES), F32) for _ in range(shifts)))
            packed = jnp.zeros((SUBS, LANES), F32)
            for r in range(shifts):
                packed = jnp.where(lane == hist_len * r + sub, jnp.sum(acc[r], axis=1, keepdims=True), packed)
            stack_row[pl.ds(in_stack, 1)] = (jnp.sum(packed, axis=0, keepdims=True) + slot_row)[None]
            pl.semaphore_wait(barrier, sum(group[0] - 1 for group in groups))
        else:
            slot = slot_index[iteration - 1]
            replaced = sub == slot

            def refresh(step, acc):
                for u in range(8):
                    t = step * 8 + u
                    new_res = jnp.where(replaced, fresh[pl.ds(t, 1), :], res[:, lane_tile(t)])
                    new_rho = jnp.where(replaced, density_out[pl.ds(t, 1), :], rho[:, lane_tile(t)])
                    res[:, lane_tile(t)] = new_res
                    rho[:, lane_tile(t)] = new_rho
                    acc = acc + fresh_w[pl.ds(t, 1), :] * new_res
                return acc

            acc = lax.fori_loop(0, tiles // 8, refresh, jnp.zeros((SUBS, LANES), F32))
            packed = jnp.where(lane == sub, jnp.sum(acc, axis=1, keepdims=True), 0.0)
            stack_row[pl.ds(in_stack, 1)] = jnp.sum(packed, axis=0, keepdims=True)[None]
        wait = exchange(stack_row, stack_group)
        if iteration == 0:
            wait_ids = exchange(id_rows, sheet_group)

        if iteration == 0:
            loads[2].wait()
        weigh()
        if iteration == 0:
            mine = hist_all.at[in_stack]
            for pair in range(hist_len // 2):
                turned = jnp.concatenate(
                    [
                        turn(hist_moments[(2 * pair + h) * rows : (2 * pair + h + 1) * rows], -32 * q)
                        for h in range(2)
                        for q in range(4)
                    ],
                    axis=0,
                )
                mine[pair] = jnp.transpose(turned)[0:harmonics]
            passed, across = channel(), channel()
            sibling = stack_peer((0, 1))
            steps = [step for step in stack_group[3] if not step[1]]
            for k, step in enumerate(steps):
                copy_to(mine, mine, across, stack_peer(step)[1], pass_sem.at[k]).start()
            copy_to(mine, mine, passed, sibling[1]).start()
            drained(hist_all.at[pl.ds(0, planes - 1)], across)
            wait_passed = waiter(hist_all, hist_all, passed, planes)
        else:
            fresh_rows = hist_moments[0:rows]
            slot_vec = jnp.zeros((rows, LANES), jnp.int32) + slot
            for i in range(1, hist_len):
                fresh_rows = jnp.where(slot_vec == i, hist_moments[i * rows : (i + 1) * rows], fresh_rows)
            turned = jnp.concatenate([turn(fresh_rows, -32 * q - 16 * h) for h in range(2) for q in range(4)], axis=0)
            new_moment = fresh_all.at[iteration - 1]
            new_moment[pl.ds(in_stack, 1)] = jnp.transpose(turned)[0 : 2 * SUBS][None]
            wait_fresh = exchange(new_moment, stack_group)

        wait()
        sheet_row[pl.ds(in_sheet, 1)] = total(stack_row, stack)[None]
        wait = exchange(sheet_row, sheet_group)

        if iteration == 0:
            ids = jnp.concatenate([stack_row[k] for k in range(stack)] * (LANES // stack), axis=0)
            ids = jnp.transpose(ids)
            for k in range(stack):
                source_cols[k * batches : (k + 1) * batches] = jnp.broadcast_to(
                    ids[half : half + batches, k : k + 1], (batches, LANES)
                )
            wait_ids()

            def fill(lanes, wanted):
                for k in range(mask.shape[0] // (2 * SUBS)):
                    at = slice(2 * SUBS * k, 2 * SUBS * (k + 1))
                    mask[at, lanes] = jnp.where(source_cols[at] == wanted, 1.0, 0.0).astype(jnp.bfloat16)

            @pl.loop(0, near_lanes // LANES)
            def _(t):
                pair = jnp.where(low_row, pltpu.roll(id_rows[2 * t], half, 1), id_rows[2 * t + 1])
                fill(lane_tile(t), pair)

            @pl.loop(0, sheet * share // LANES)
            def _(t):
                at = t * (LANES // share) + lane_row // share
                member = (at % spans) * cores + my_core
                held = member * owned + ((at // spans) * depth + lax.rem(my_plane, depth)) * share
                fill(lane_tile(t + near_lanes // LANES), (held + lane_row % share).astype(F32))

            for load in loads[3:]:
                load.wait()

        wait()
        row = total(sheet_row, sheet)
        if iteration == 0:
            entry = [[None] * (i + 1) for i in range(hist_len)]
            for i in range(hist_len):
                for j in range(i + 1):
                    r = i - j
                    at = hist_len * r + i if r < shifts else hist_len * (hist_len - r) + j
                    entry[i][j] = splat(row, at)
        else:
            news = [splat(row, k) for k in range(hist_len)]
            slot_vec = jnp.zeros((1, LANES), jnp.int32) + slot
            entry = [
                [
                    jnp.where(slot_vec == i, news[j], jnp.where(slot_vec == j, news[i], entry[i][j]))
                    for j in range(i + 1)
                ]
                for i in range(hist_len)
            ]
        coeffs = solve_coeffs(entry, hist_len)
        coeff_col = jnp.zeros((SUBS, LANES), F32)
        for i in range(hist_len):
            coeff_col = jnp.where(sub == i, coeffs[i], coeff_col)

        if iteration == 0:
            for k, step in enumerate(steps):
                back = ((planes - step[0]) % planes, 0)
                block = hist_all.at[stack_peer(back)[0]]
                pltpu.make_async_copy(block, block, pass_sem.at[k]).wait()
                copy_to(block, block, passed, sibling[1]).start()
            wait_passed()
            old = coeffs
        else:
            wait_fresh()
            old = [jnp.where(slot_vec == i, 0.0, coeffs[i]) for i in range(hist_len)]
            new = coeffs[0]
            for i in range(1, hist_len):
                new = jnp.where(slot_vec == i, coeffs[i], new)

        gains = [jnp.where(low_row, old[2 * pair], old[2 * pair + 1]) for pair in range(hist_len // 2)]

        def mixed(at):
            top = tree(gains[pair] * hist_all[at, pair, 0:24] for pair in range(hist_len // 2))
            end = tree(gains[pair] * hist_all[at, pair, 24:25] for pair in range(hist_len // 2))
            return jnp.concatenate([top, jnp.broadcast_to(end, (SUBS, LANES))], axis=0)

        blocks = []
        for k in range(0, stack, 2):
            one, two = mixed(k), mixed(k + 1)
            block = jnp.where(low_wide, one, two) + pltpu.roll(jnp.where(low_wide, two, one), half, 1)
            if iteration:
                one, two = new_moment[k], new_moment[k + 1]
                upper = jnp.where(low, one, pltpu.roll(two, half, 1))
                lower = jnp.where(low, pltpu.roll(one, half, 1), two)
                block = block + new * jnp.concatenate([upper, lower], axis=0)
            blocks.append(block)
        everywhere = jnp.concatenate(blocks, axis=1)
        pieces = jnp.concatenate(split(everywhere), axis=0).astype(jnp.bfloat16)

        def gathered(first, count):
            out = jnp.dot(
                pieces, mask[:, pl.ds(pl.multiple_of(first, count), count)], preferred_element_type=F32
            )
            return out[0:32] + out[32:64] + out[64:96]

        if last:
            many = 2 * LANES // share
            each = LANES // share
            send, wait_own = scatter(own_send, own_recv, sheet_group)
            for first in range(0, sheet, many):
                out = gathered(near_lanes + first * share, many * share)
                for k in range(many):
                    tile = out[:, k // each * LANES : (k // each + 1) * LANES]
                    kept = jnp.zeros((SUBS, LANES), F32)
                    for g in range(4):
                        piece = tile[g * SUBS : (g + 1) * SUBS]
                        kept = jnp.where(quarter == g, turn(piece, (g - k % each) * 32), kept)
                    own_send[first + k] = kept
            own_recv[pl.ds(in_sheet, 1)] = own_send[pl.ds(in_sheet, 1)]
            for step in sheet_group[3]:
                send(step)

        send, wait = scatter(sent, received, sheet_group)
        for line_step in sorted(range(lines), key=lambda step: -ring(step, lines)):
            first = lax.rem(my_line + line_step, lines) * spans
            out = gathered(first * batches, spans * batches)
            for k in range(0, spans, 2):
                upper = out[0:16, k * batches : (k + 2) * batches]
                lower = out[16:32, k * batches : (k + 2) * batches]
                sent[first + k] = jnp.where(low, upper, pltpu.roll(lower, half, 1))
                sent[first + k + 1] = jnp.where(low, pltpu.roll(upper, half, 1), lower)
            for step in sheet_group[3]:
                if step[0] == line_step:
                    send(step)
        received[pl.ds(in_sheet, 1)] = sent[pl.ds(in_sheet, 1)]

        def base_step(step, carry):
            for u in range(8):
                t = step * 8 + u
                part = coeff_col * (rho[:, lane_tile(t)] + mixing_beta * res[:, lane_tile(t)])
                base_rows[pl.ds(t, 1), :] = jnp.sum(part, axis=0, keepdims=True)
            return carry

        lax.fori_loop(0, tiles // 8, base_step, 0)

        if last:
            wait_own()
            chunks[pl.ds(my_share, 1)] = (total(own_recv, sheet) * scale)[None]
            wait_chunks = exchange(chunks, share_group)

        wait()
        summed = total(received, sheet)
        at_batch = jnp.concatenate([summed, pltpu.roll(summed, half, 1)], axis=0) * scale
        comp = lax.broadcasted_iota(jnp.int32, (32, LANES), 0)
        degree = sum((comp >= (l + 1) * (l + 1)).astype(F32) for l in range(4))
        damped = jnp.where(comp < harmonics, at_batch * (mixing_beta / (1.0 + degree)), 0.0)

        def density_step(step, ahead):
            for u in range(16):
                b = step * 16 + u
                col = jnp.broadcast_to(ahead[:, u : u + 1], (32, LANES))
                for v in range(per_batch):
                    t = b * per_batch + v
                    part = col[24:32] * basis[24:25, lane_tile(t)]
                    for g in range(3):
                        part = part + col[g * SUBS : (g + 1) * SUBS] * basis[g * SUBS : (g + 1) * SUBS, lane_tile(t)]
                    correct[pl.ds(t, 1), :] = jnp.sum(part, axis=0, keepdims=True)
            return pltpu.roll(ahead, LANES - 16, 1)

        lax.fori_loop(0, batches // 16, density_step, damped)
        density = base_rows[...] - correct[...]
        density_out[...] = density
        if last:
            wait_chunks()
            each = LANES // share
            for t in range(owned // LANES):
                held = [chunks[t * each + k] for k in range(each)]
                for g in range(4):
                    tile = jnp.zeros((SUBS, LANES), F32)
                    for k in range(each):
                        tile = jnp.where(quarter == k, turn(held[k], (k - g) * 32), tile)
                    top = min(SUBS, harmonics - g * SUBS)
                    moments_out[g * SUBS : g * SUBS + top, t * LANES : (t + 1) * LANES] = tile[0:top]
        else:
            new = target[...] + coupling[...] * jnp.tanh(density) - density
            fresh[...] = new
            fresh_w[...] = new * w[...]
    for src, sem in sends:
        pltpu.make_async_copy(src, src, sem).wait()


def finish(density, moments, density_out, moments_out):
    density_out[...] = density[...]
    moments_out[...] = moments[...]


def local(weights, target, coupling, multipole_basis, rho_hist, res_hist, batch_atom, owner_slot, slot_index):
    harmonics, points = multipole_basis.shape
    hist_len = res_hist.shape[0]
    batches = batch_atom.shape[0]
    groups = lax.axis_size("grid")
    members = lax.axis_size("atom")
    lines, cores = 4, 2
    planes = groups // lines
    spans = members // cores
    stack, sheet = planes * cores, lines * spans
    shares = 4 * lines
    owned = owner_slot.shape[0] // members
    scale = 1.0 / math.sqrt(points * groups // owned)
    iters = slot_index.shape[0]
    cfg = (iters, hist_len, harmonics, batches, points // batches, owned, planes, lines, spans, cores, scale)
    tiles = points // LANES
    flat = (tiles, LANES)
    kinds = 3 * iters + 5 + (iters - 1)
    any_space = pl.BlockSpec(memory_space=pl.ANY)
    smem = pl.BlockSpec(memory_space=pltpu.SMEM)
    vmem = pl.BlockSpec(memory_space=pltpu.VMEM)
    density, moments = pl.pallas_call(
        functools.partial(kernel, cfg),
        out_shape=(jax.ShapeDtypeStruct(flat, F32), jax.ShapeDtypeStruct((harmonics, owned), F32)),
        in_specs=[smem] * 3 + [any_space] * 6,
        out_specs=(vmem, vmem),
        scratch_shapes=[
            pltpu.VMEM(flat, F32),
            pltpu.VMEM(flat, F32),
            pltpu.VMEM(flat, F32),
            pltpu.VMEM((harmonics, points), F32),
            pltpu.VMEM((hist_len, points), F32),
            pltpu.VMEM((hist_len, points), F32),
            pltpu.VMEM(flat, F32),
            pltpu.VMEM(flat, F32),
            pltpu.VMEM((iters, stack, 1, LANES), F32),
            pltpu.VMEM((iters, sheet, 1, LANES), F32),
            pltpu.VMEM((sheet, 1, LANES), F32),
            pltpu.VMEM((stack, hist_len // 2, harmonics, LANES), F32),
            pltpu.VMEM((iters - 1, stack, 2 * SUBS, LANES), F32),
            pltpu.VMEM((iters, sheet, 2 * SUBS, LANES), F32),
            pltpu.VMEM((iters, sheet, 2 * SUBS, LANES), F32),
            pltpu.VMEM((sheet, SUBS, LANES), F32),
            pltpu.VMEM((sheet, SUBS, LANES), F32),
            pltpu.VMEM((shares, SUBS, LANES), F32),
            pltpu.VMEM((stack * batches, LANES), F32),
            pltpu.VMEM((stack * batches, sheet * (batches + owned // shares)), jnp.bfloat16),
            pltpu.VMEM((batches // 4 * hist_len, LANES), F32),
            pltpu.VMEM(flat, F32),
            pltpu.VMEM(flat, F32),
            pltpu.SemaphoreType.DMA((6,)),
            pltpu.SemaphoreType.DMA((kinds,)),
            pltpu.SemaphoreType.DMA((kinds,)),
            pltpu.SemaphoreType.DMA((planes - 1,)),
        ],
        compiler_params=pltpu.CompilerParams(
            collective_id=0, has_side_effects=True, vmem_limit_bytes=67043328
        ),
    )(
        batch_atom,
        owner_slot,
        slot_index,
        weights.reshape(flat),
        target.reshape(flat),
        coupling.reshape(flat),
        multipole_basis,
        rho_hist,
        res_hist,
    )
    density, moments = pl.pallas_call(
        finish,
        out_shape=(jax.ShapeDtypeStruct(flat, F32), jax.ShapeDtypeStruct((harmonics, owned), F32)),
        in_specs=[vmem] * 2,
        out_specs=(vmem, vmem),
    )(density, moments)
    return density.reshape(points), moments


def solution(mesh):
    both = ("grid", "atom")
    placed = (P(both), P(both), P(both), P(None, both), P(None, both), P(None, both), P(both), P(), P())
    return jax.shard_map(
        local,
        mesh=mesh,
        in_specs=placed,
        out_specs=(P(both), P(None, "atom")),
        check_vma=False,
    )
```

time: 63.5 us -> 53.1 us (0.84)
  the two profiles are of different devices: /device:TPU:1 before, /device:TPU:2 now
where the time goes in v3:
time: 53.1 us; the launch traced here: 52.9 us
  Pallas kernels  52.2 us (98%)
  between operations  0.64 us (1%)
    pallas_call x1, Pallas kernels, local(): pl.pallas_call(functools.partial(kernel, cfg), out_shape=(jax.ShapeDtypeS...  50.7 us
    pallas_call x1, Pallas kernels, local(): pl.pallas_call(finish, out_shape=(jax.ShapeDtypeStruct(flat, F32), jax.Sh...  1.53 us

profile of v3, /device:TPU:2, one launch (start us, length us, event | category | flops | bytes accessed | tf_op | source)
XLA Modules:
  0.0 52.9 jit_solution(17867293857469360695)
XLA Ops:
  0.6 50.7 %shard_map.104 = (f32[128,128]{1,0:T(8,128)}, f32[25,512]{1,0:T(8,128)}) custom-call(s32[64]{0:T(128)} %batch_atom.1, s32[4096]{0:T(1024)} %owner_slot.1, s32[2]{0:T(128)} %slot_index.1, f32[128,128]{1,0:T(8,128)} %bitcast.4, f32[128,128]{1,0:T(8,128)} %bitcast.5, f32[128,128]{1,0:T(8,128)} %bitcast.6, f32[25,16384]{1,0:T(8,128)} %basis_hbm.1, ...), custom_call_target="tpu_custom_call" | custom-call | tf_op jit(solution)/shard_map/pallas_call | solution.py:554
  51.3 1.5 %shard_map.105 = (f32[128,128]{1,0:T(8,128)}, f32[25,512]{1,0:T(8,128)}) custom-call(f32[128,128]{1,0:T(8,128)} %get-tuple-element.6.density, f32[25,512]{1,0:T(8,128)} %get-tuple-element.7.moments), custom_call_target="tpu_custom_call" | custom-call | tf_op jit(solution)/shard_map/pallas_call | solution.py:602

commit v4 on v3

--- a/solution.py
+++ b/solution.py
@@ -56,9 +56,9 @@
 
 def kernel(
     cfg,
-    batch_atom,
-    owner_slot,
-    slot_index,
+    batch_atom_hbm,
+    owner_slot_hbm,
+    slot_index_hbm,
     w_hbm,
     target_hbm,
     coupling_hbm,
@@ -90,6 +90,9 @@
     hist_moments,
     base_rows,
     correct,
+    batch_atom,
+    owner_slot,
+    slot_index,
     load_sem,
     send_sem,
     recv_sem,
@@ -140,19 +143,32 @@
     sheet_group = (sheet, in_sheet, sheet_peer, far_first(lines, spans))
     share_group = (shares, my_share, share_peer, far_first(lines, depth))
     groups = (stack_group, sheet_group, share_group)
+    first_half = pl.ds(0, tiles * LANES // 2)
+    second_half = pl.ds(tiles * LANES // 2, tiles * LANES // 2)
+    loads = [
+        pltpu.make_async_copy(src, dst, load_sem.at[k])
+        for k, (src, dst) in enumerate(
+            (
+                (w_hbm, w),
+                (res_hbm.at[:, first_half], res.at[:, first_half]),
+                (res_hbm.at[:, second_half], res.at[:, second_half]),
+                (batch_atom_hbm, batch_atom),
+                (owner_slot_hbm, owner_slot),
+                (basis_hbm, basis),
+                (slot_index_hbm, slot_index),
+                (rho_hbm, rho),
+                (target_hbm, target),
+                (coupling_hbm, coupling),
+            )
+        )
+    ]
+    for load in loads:
+        load.start()
+
     barrier = pltpu.get_barrier_semaphore()
     for _, _, peer, steps in groups:
         for step in steps:
             pl.semaphore_signal(barrier, inc=1, device_id=peer(step)[1], device_id_type=MESH)
-
-    loads = [
-        pltpu.make_async_copy(src, dst, load_sem.at[k])
-        for k, (src, dst) in enumerate(
-            ((res_hbm, res), (w_hbm, w), (basis_hbm, basis), (rho_hbm, rho), (target_hbm, target), (coupling_hbm, coupling))
-        )
-    ]
-    for load in loads:
-        load.start()
 
     lane = lax.broadcasted_iota(jnp.int32, (SUBS, LANES), 1)
     sub = lax.broadcasted_iota(jnp.int32, (SUBS, LANES), 0)
@@ -161,11 +177,6 @@
     low_row = lane_row < half
     low = lax.broadcasted_iota(jnp.int32, (2 * SUBS, LANES), 1) < half
     low_wide = lax.broadcasted_iota(jnp.int32, (32, LANES), 1) < half
-
-    slot_row = jnp.zeros((1, LANES), F32)
-    for b in range(batches):
-        slot_row = jnp.where(lane_row == half + b, owner_slot[batch_atom[b]].astype(F32), slot_row)
-    id_rows[pl.ds(in_sheet, 1)] = slot_row[None]
 
     def lane_tile(t):
         return pl.ds(pl.multiple_of(t * LANES, LANES), LANES)
@@ -229,10 +240,10 @@
         return jnp.broadcast_to(row[:, k : k + 1], (1, LANES))
 
     def weigh():
-        @pl.loop(0, rows // 2)
+        @pl.loop(0, rows // 4)
         def _(step):
-            for u in range(2):
-                r = step * 2 + u
+            for u in range(4):
+                r = step * 4 + u
                 xs, ys = [], []
                 for q in range(4):
                     b = q * rows + r
@@ -281,7 +292,16 @@
                         acc[r] = acc[r] + y * (pltpu.roll(x, r, 0) if r else x)
                 return tuple(acc)
 
-            acc = lax.fori_loop(0, tiles // 8, gram, tuple(jnp.zeros((SUBS, LANES), F32) for _ in range(shifts)))
+            acc = tuple(jnp.zeros((SUBS, LANES), F32) for _ in range(shifts))
+            acc = lax.fori_loop(0, tiles // 16, gram, acc)
+            loads[2].wait()
+            acc = lax.fori_loop(tiles // 16, tiles // 8, gram, acc)
+            loads[3].wait()
+            loads[4].wait()
+            slot_row = jnp.zeros((1, LANES), F32)
+            for b in range(batches):
+                slot_row = jnp.where(lane_row == half + b, owner_slot[batch_atom[b]].astype(F32), slot_row)
+            id_rows[pl.ds(in_sheet, 1)] = slot_row[None]
             packed = jnp.zeros((SUBS, LANES), F32)
             for r in range(shifts):
                 packed = jnp.where(lane == hist_len * r + sub, jnp.sum(acc[r], axis=1, keepdims=True), packed)
@@ -309,7 +329,7 @@
             wait_ids = exchange(id_rows, sheet_group)
 
         if iteration == 0:
-            loads[2].wait()
+            loads[5].wait()
         weigh()
         if iteration == 0:
             mine = hist_all.at[in_stack]
@@ -324,11 +344,25 @@
                 )
                 mine[pair] = jnp.transpose(turned)[0:harmonics]
             passed, across = channel(), channel()
-            sibling = stack_peer((0, 1))
-            steps = [step for step in stack_group[3] if not step[1]]
-            for k, step in enumerate(steps):
-                copy_to(mine, mine, across, stack_peer(step)[1], pass_sem.at[k]).start()
-            copy_to(mine, mine, passed, sibling[1]).start()
+            sibling = stack_peer((0, 1))[1]
+            far = planes // 2
+            near_steps = [(sign * hop) % planes for hop in (far // 2, 1) for sign in (1, -1)]
+
+            def block_of(step):
+                return hist_all.at[stack_peer((-step % planes, 0))[0]]
+
+            def move(block, step, arrival):
+                copy_to(block, block, across, stack_peer((step % planes, 0))[1], pass_sem.at[arrival]).start()
+
+            def landed(block, arrival):
+                pltpu.make_async_copy(block, block, pass_sem.at[arrival]).wait()
+
+            def pass_on(block):
+                copy_to(block, block, passed, sibling).start()
+
+            for step in near_steps:
+                move(mine, step, step)
+            pass_on(mine)
             drained(hist_all.at[pl.ds(0, planes - 1)], across)
             wait_passed = waiter(hist_all, hist_all, passed, planes)
         else:
@@ -371,8 +405,18 @@
                 held = member * owned + ((at // spans) * depth + lax.rem(my_plane, depth)) * share
                 fill(lane_tile(t + near_lanes // LANES), (held + lane_row % share).astype(F32))
 
-            for load in loads[3:]:
+            for load in loads[6:]:
                 load.wait()
+
+        if iteration == 0:
+            hops = far // 2
+            for sign in (1, -1):
+                block = block_of(sign * hops)
+                landed(block, sign * hops % planes)
+                part = pl.ds(0 if sign > 0 else hist_len // 4, hist_len // 4)
+                move(block.at[part], sign * hops, far)
+                move(block, sign * (far - 1 - hops), sign * (far - 1) % planes)
+                pass_on(block)
 
         wait()
         row = total(sheet_row, sheet)
@@ -399,11 +443,10 @@
             coeff_col = jnp.where(sub == i, coeffs[i], coeff_col)
 
         if iteration == 0:
-            for k, step in enumerate(steps):
-                back = ((planes - step[0]) % planes, 0)
-                block = hist_all.at[stack_peer(back)[0]]
-                pltpu.make_async_copy(block, block, pass_sem.at[k]).wait()
-                copy_to(block, block, passed, sibling[1]).start()
+            for step in (1, planes - 1, far - 1, planes - far + 1, far):
+                block = block_of(step)
+                landed(block, step)
+                pass_on(block)
             wait_passed()
             old = coeffs
         else:
@@ -548,13 +591,12 @@
     tiles = points // LANES
     flat = (tiles, LANES)
     kinds = 3 * iters + 5 + (iters - 1)
-    any_space = pl.BlockSpec(memory_space=pl.ANY)
-    smem = pl.BlockSpec(memory_space=pltpu.SMEM)
+    any_space = pl.BlockSpec(memory_space=pltpu.HBM)
     vmem = pl.BlockSpec(memory_space=pltpu.VMEM)
     density, moments = pl.pallas_call(
         functools.partial(kernel, cfg),
         out_shape=(jax.ShapeDtypeStruct(flat, F32), jax.ShapeDtypeStruct((harmonics, owned), F32)),
-        in_specs=[smem] * 3 + [any_space] * 6,
+        in_specs=[any_space] * 9,
         out_specs=(vmem, vmem),
         scratch_shapes=[
             pltpu.VMEM(flat, F32),
@@ -580,30 +622,39 @@
             pltpu.VMEM((batches // 4 * hist_len, LANES), F32),
             pltpu.VMEM(flat, F32),
             pltpu.VMEM(flat, F32),
-            pltpu.SemaphoreType.DMA((6,)),
+            pltpu.SMEM(batch_atom.shape, jnp.int32),
+            pltpu.SMEM(owner_slot.shape, jnp.int32),
+            pltpu.SMEM(slot_index.shape, jnp.int32),
+            pltpu.SemaphoreType.DMA((10,)),
             pltpu.SemaphoreType.DMA((kinds,)),
             pltpu.SemaphoreType.DMA((kinds,)),
-            pltpu.SemaphoreType.DMA((planes - 1,)),
+            pltpu.SemaphoreType.DMA((planes,)),
         ],
         compiler_params=pltpu.CompilerParams(
-            collective_id=0, has_side_effects=True, vmem_limit_bytes=67043328
+            collective_id=0, has_side_effects=True, vmem_limit_bytes=16777216
         ),
     )(
-        batch_atom,
-        owner_slot,
-        slot_index,
-        weights.reshape(flat),
-        target.reshape(flat),
-        coupling.reshape(flat),
-        multipole_basis,
-        rho_hist,
-        res_hist,
+        *(
+            pltpu.with_memory_space_constraint(array, pltpu.HBM)
+            for array in (
+                batch_atom,
+                owner_slot,
+                slot_index,
+                weights.reshape(flat),
+                target.reshape(flat),
+                coupling.reshape(flat),
+                multipole_basis,
+                rho_hist,
+                res_hist,
+            )
+        )
     )
     density, moments = pl.pallas_call(
         finish,
         out_shape=(jax.ShapeDtypeStruct(flat, F32), jax.ShapeDtypeStruct((harmonics, owned), F32)),
         in_specs=[vmem] * 2,
         out_specs=(vmem, vmem),
+        compiler_params=pltpu.CompilerParams(vmem_limit_bytes=1048576),
     )(density, moments)
     return density.reshape(points), moments
 

time: 53.1 us -> 48.4 us (0.911)
  Pallas kernels: 52.2 us -> 47.7 us
    pallas_call x1, Pallas kernels: 50.7 us -> 47 us  [local(): pl.pallas_call(functools.partial(kernel, cfg), out_shape=(jax.ShapeDtypeS...]
    pallas_call x1, Pallas kernels: 1.53 us -> 0.66 us  [local(): pl.pallas_call(finish, out_shape=(jax.ShapeDtypeStruct(flat, F32), jax.Sh...]
where the time goes in v4:
time: 48.4 us; the launch traced here: 48.3 us
  Pallas kernels  47.7 us (99%)
  between operations  0.64 us (1%)
    pallas_call x1, Pallas kernels, local(): pl.pallas_call(functools.partial(kernel, cfg), out_shape=(jax.ShapeDtypeS...  47 us

profile of v4, /device:TPU:2, one launch (start us, length us, event | category | flops | bytes accessed | tf_op | source)
XLA Modules:
  0.0 48.3 jit_solution(5796521979462777250)
XLA Ops:
  0.6 47.0 %shard_map.104 = (f32[128,128]{1,0:T(8,128)S(1)}, f32[25,512]{1,0:T(8,128)S(1)}) custom-call(s32[64]{0:T(128)} %batch_atom_hbm.1, s32[4096]{0:T(1024)} %owner_slot_hbm.1, s32[2]{0:T(128)} %slot_index_hbm.1, f32[128,128]{1,0:T(8,128)} %bitcast.4, f32[128,128]{1,0:T(8,128)} %bitcast.5, f32[128,128]{1,0:T(8,128)} %bitcast.6, f32[25,16384]{1,0:T(8,128)} %basis_hbm.1, ...), custom_call_target="tpu_custom_call" | custom-call | tf_op jit(solution)/shard_map/pallas_call | solution.py:596
  47.6 0.7 %shard_map.105 = (f32[128,128]{1,0:T(8,128)}, f32[25,512]{1,0:T(8,128)}) custom-call(f32[128,128]{1,0:T(8,128)S(1)} %get-tuple-element.6.density, f32[25,512]{1,0:T(8,128)S(1)} %get-tuple-element.7.moments), custom_call_target="tpu_custom_call" | custom-call | tf_op jit(solution)/shard_map/pallas_call | solution.py:652

commit v5 on v4

--- a/solution.py
+++ b/solution.py
@@ -142,7 +142,12 @@
     stack_group = (stack, in_stack, stack_peer, far_first(planes, cores))
     sheet_group = (sheet, in_sheet, sheet_peer, far_first(lines, spans))
     share_group = (shares, my_share, share_peer, far_first(lines, depth))
-    groups = (stack_group, sheet_group, share_group)
+    groups = (stack_group, sheet_group)
+    barrier = pltpu.get_barrier_semaphore()
+    for _, _, peer, steps in groups:
+        for step in steps:
+            pl.semaphore_signal(barrier, inc=1, device_id=peer(step)[1], device_id_type=MESH)
+
     first_half = pl.ds(0, tiles * LANES // 2)
     second_half = pl.ds(tiles * LANES // 2, tiles * LANES // 2)
     loads = [
@@ -164,11 +169,6 @@
     ]
     for load in loads:
         load.start()
-
-    barrier = pltpu.get_barrier_semaphore()
-    for _, _, peer, steps in groups:
-        for step in steps:
-            pl.semaphore_signal(barrier, inc=1, device_id=peer(step)[1], device_id_type=MESH)
 
     lane = lax.broadcasted_iota(jnp.int32, (SUBS, LANES), 1)
     sub = lax.broadcasted_iota(jnp.int32, (SUBS, LANES), 0)
@@ -306,32 +306,8 @@
             for r in range(shifts):
                 packed = jnp.where(lane == hist_len * r + sub, jnp.sum(acc[r], axis=1, keepdims=True), packed)
             stack_row[pl.ds(in_stack, 1)] = (jnp.sum(packed, axis=0, keepdims=True) + slot_row)[None]
-            pl.semaphore_wait(barrier, sum(group[0] - 1 for group in groups))
-        else:
-            slot = slot_index[iteration - 1]
-            replaced = sub == slot
-
-            def refresh(step, acc):
-                for u in range(8):
-                    t = step * 8 + u
-                    new_res = jnp.where(replaced, fresh[pl.ds(t, 1), :], res[:, lane_tile(t)])
-                    new_rho = jnp.where(replaced, density_out[pl.ds(t, 1), :], rho[:, lane_tile(t)])
-                    res[:, lane_tile(t)] = new_res
-                    rho[:, lane_tile(t)] = new_rho
-                    acc = acc + fresh_w[pl.ds(t, 1), :] * new_res
-                return acc
-
-            acc = lax.fori_loop(0, tiles // 8, refresh, jnp.zeros((SUBS, LANES), F32))
-            packed = jnp.where(lane == sub, jnp.sum(acc, axis=1, keepdims=True), 0.0)
-            stack_row[pl.ds(in_stack, 1)] = jnp.sum(packed, axis=0, keepdims=True)[None]
-        wait = exchange(stack_row, stack_group)
-        if iteration == 0:
-            wait_ids = exchange(id_rows, sheet_group)
-
-        if iteration == 0:
             loads[5].wait()
-        weigh()
-        if iteration == 0:
+            weigh()
             mine = hist_all.at[in_stack]
             for pair in range(hist_len // 2):
                 turned = jnp.concatenate(
@@ -343,6 +319,29 @@
                     axis=0,
                 )
                 mine[pair] = jnp.transpose(turned)[0:harmonics]
+            pl.semaphore_wait(barrier, sum(group[0] - 1 for group in groups))
+        else:
+            slot = slot_index[iteration - 1]
+            replaced = sub == slot
+
+            def refresh(step, acc):
+                for u in range(8):
+                    t = step * 8 + u
+                    new_res = jnp.where(replaced, fresh[pl.ds(t, 1), :], res[:, lane_tile(t)])
+                    new_rho = jnp.where(replaced, density_out[pl.ds(t, 1), :], rho[:, lane_tile(t)])
+                    res[:, lane_tile(t)] = new_res
+                    rho[:, lane_tile(t)] = new_rho
+                    acc = acc + fresh_w[pl.ds(t, 1), :] * new_res
+                return acc
+
+            acc = lax.fori_loop(0, tiles // 8, refresh, jnp.zeros((SUBS, LANES), F32))
+            packed = jnp.where(lane == sub, jnp.sum(acc, axis=1, keepdims=True), 0.0)
+            stack_row[pl.ds(in_stack, 1)] = jnp.sum(packed, axis=0, keepdims=True)[None]
+        wait = exchange(stack_row, stack_group)
+        if iteration == 0:
+            wait_ids = exchange(id_rows, sheet_group)
+
+        if iteration == 0:
             passed, across = channel(), channel()
             sibling = stack_peer((0, 1))[1]
             far = planes // 2
@@ -366,6 +365,7 @@
             drained(hist_all.at[pl.ds(0, planes - 1)], across)
             wait_passed = waiter(hist_all, hist_all, passed, planes)
         else:
+            weigh()
             fresh_rows = hist_moments[0:rows]
             slot_vec = jnp.zeros((rows, LANES), jnp.int32) + slot
             for i in range(1, hist_len):
@@ -378,35 +378,6 @@
         wait()
         sheet_row[pl.ds(in_sheet, 1)] = total(stack_row, stack)[None]
         wait = exchange(sheet_row, sheet_group)
-
-        if iteration == 0:
-            ids = jnp.concatenate([stack_row[k] for k in range(stack)] * (LANES // stack), axis=0)
-            ids = jnp.transpose(ids)
-            for k in range(stack):
-                source_cols[k * batches : (k + 1) * batches] = jnp.broadcast_to(
-                    ids[half : half + batches, k : k + 1], (batches, LANES)
-                )
-            wait_ids()
-
-            def fill(lanes, wanted):
-                for k in range(mask.shape[0] // (2 * SUBS)):
-                    at = slice(2 * SUBS * k, 2 * SUBS * (k + 1))
-                    mask[at, lanes] = jnp.where(source_cols[at] == wanted, 1.0, 0.0).astype(jnp.bfloat16)
-
-            @pl.loop(0, near_lanes // LANES)
-            def _(t):
-                pair = jnp.where(low_row, pltpu.roll(id_rows[2 * t], half, 1), id_rows[2 * t + 1])
-                fill(lane_tile(t), pair)
-
-            @pl.loop(0, sheet * share // LANES)
-            def _(t):
-                at = t * (LANES // share) + lane_row // share
-                member = (at % spans) * cores + my_core
-                held = member * owned + ((at // spans) * depth + lax.rem(my_plane, depth)) * share
-                fill(lane_tile(t + near_lanes // LANES), (held + lane_row % share).astype(F32))
-
-            for load in loads[6:]:
-                load.wait()
 
         if iteration == 0:
             hops = far // 2
@@ -417,6 +388,34 @@
                 move(block.at[part], sign * hops, far)
                 move(block, sign * (far - 1 - hops), sign * (far - 1) % planes)
                 pass_on(block)
+
+            ids = jnp.concatenate([stack_row[k] for k in range(stack)] * (LANES // stack), axis=0)
+            ids = jnp.transpose(ids)
+            for k in range(stack):
+                source_cols[k * batches : (k + 1) * batches] = jnp.broadcast_to(
+                    ids[half : half + batches, k : k + 1], (batches, LANES)
+                )
+            wait_ids()
+
+            def fill(lanes, wanted):
+                for k in range(mask.shape[0] // (2 * SUBS)):
+                    at = slice(2 * SUBS * k, 2 * SUBS * (k + 1))
+                    mask[at, lanes] = jnp.where(source_cols[at] == wanted, 1.0, 0.0).astype(jnp.bfloat16)
+
+            @pl.loop(0, near_lanes // LANES)
+            def _(t):
+                pair = jnp.where(low_row, pltpu.roll(id_rows[2 * t], half, 1), id_rows[2 * t + 1])
+                fill(lane_tile(t), pair)
+
+            @pl.loop(0, sheet * share // LANES)
+            def _(t):
+                at = t * (LANES // share) + lane_row // share
+                member = (at % spans) * cores + my_core
+                held = member * owned + ((at // spans) * depth + lax.rem(my_plane, depth)) * share
+                fill(lane_tile(t + near_lanes // LANES), (held + lane_row % share).astype(F32))
+
+            for load in loads[6:]:
+                load.wait()
 
         wait()
         row = total(sheet_row, sheet)

time: 48.4 us -> 47.5 us (0.981)
  Pallas kernels: 47.7 us -> 46.8 us
    pallas_call x1, Pallas kernels: 47 us -> 46.1 us  [local(): pl.pallas_call(functools.partial(kernel, cfg), out_shape=(jax.ShapeDtypeS...]
where the time goes in v5:
time: 47.5 us; the launch traced here: 47.4 us
  Pallas kernels  46.8 us (99%)
  between operations  0.64 us (1%)
    pallas_call x1, Pallas kernels, local(): pl.pallas_call(functools.partial(kernel, cfg), out_shape=(jax.ShapeDtypeS...  46.1 us

profile of v5, /device:TPU:2, one launch (start us, length us, event | category | flops | bytes accessed | tf_op | source)
XLA Modules:
  0.0 47.4 jit_solution(8595244390104328953)
XLA Ops:
  0.6 46.1 %shard_map.104 = (f32[128,128]{1,0:T(8,128)S(1)}, f32[25,512]{1,0:T(8,128)S(1)}) custom-call(s32[64]{0:T(128)} %batch_atom_hbm.1, s32[4096]{0:T(1024)} %owner_slot_hbm.1, s32[2]{0:T(128)} %slot_index_hbm.1, f32[128,128]{1,0:T(8,128)} %bitcast.4, f32[128,128]{1,0:T(8,128)} %bitcast.5, f32[128,128]{1,0:T(8,128)} %bitcast.6, f32[25,16384]{1,0:T(8,128)} %basis_hbm.1, ...), custom_call_target="tpu_custom_call" | custom-call | tf_op jit(solution)/shard_map/pallas_call | solution.py:595
  46.7 0.7 %shard_map.105 = (f32[128,128]{1,0:T(8,128)}, f32[25,512]{1,0:T(8,128)}) custom-call(f32[128,128]{1,0:T(8,128)S(1)} %get-tuple-element.6.density, f32[25,512]{1,0:T(8,128)S(1)} %get-tuple-element.7.moments), custom_call_target="tpu_custom_call" | custom-call | tf_op jit(solution)/shard_map/pallas_call | solution.py:651

commit v6 on v5

--- a/solution.py
+++ b/solution.py
@@ -45,9 +45,9 @@
     return [backward[i] / total for i in range(hist_len)]
 
 
-def split(x):
+def split(x, count=3):
     pieces = []
-    for _ in range(3):
+    for _ in range(count):
         piece = x.astype(jnp.bfloat16).astype(F32)
         pieces.append(piece)
         x = x - piece
@@ -148,6 +148,7 @@
         for step in steps:
             pl.semaphore_signal(barrier, inc=1, device_id=peer(step)[1], device_id_type=MESH)
 
+    quarters = [pl.ds(k * tiles * LANES // 4, tiles * LANES // 4) for k in range(4)]
     first_half = pl.ds(0, tiles * LANES // 2)
     second_half = pl.ds(tiles * LANES // 2, tiles * LANES // 2)
     loads = [
@@ -159,7 +160,7 @@
                 (res_hbm.at[:, second_half], res.at[:, second_half]),
                 (batch_atom_hbm, batch_atom),
                 (owner_slot_hbm, owner_slot),
-                (basis_hbm, basis),
+                *((basis_hbm.at[:, part], basis.at[:, part]) for part in quarters),
                 (slot_index_hbm, slot_index),
                 (rho_hbm, rho),
                 (target_hbm, target),
@@ -239,7 +240,7 @@
     def splat(row, k):
         return jnp.broadcast_to(row[:, k : k + 1], (1, LANES))
 
-    def weigh():
+    def weigh(weighted):
         @pl.loop(0, rows // 4)
         def _(step):
             for u in range(4):
@@ -248,14 +249,13 @@
                 for q in range(4):
                     b = q * rows + r
                     at = pl.ds(pl.multiple_of(b * width, width), width)
-                    gain = jnp.concatenate([w[pl.ds(b * per_batch + v, 1), :] for v in range(per_batch)], axis=1)
-                    xs.extend(split(res[:, at] * gain))
+                    xs.extend(split(weighted(b, at)))
                     ys.append(
                         jnp.concatenate([basis[0:24, at], jnp.broadcast_to(basis[24:25, at], (SUBS, width))], axis=0)
                     )
                 x = jnp.concatenate(xs, axis=0).astype(jnp.bfloat16)
                 out = None
-                for y in split(jnp.concatenate(ys, axis=0)):
+                for y in split(jnp.concatenate(ys, axis=0), 2):
                     part = lax.dot_general(
                         x, y.astype(jnp.bfloat16), (((1,), (1,)), ((), ())), preferred_element_type=F32
                     )
@@ -266,6 +266,15 @@
                     tile = jnp.where(quarter == q, block, tile)
                 hist_moments[pl.ds(r, hist_len, stride=rows), :] = tile
 
+    def batch_row(ref, b):
+        return jnp.concatenate([ref[pl.ds(b * per_batch + v, 1), :] for v in range(per_batch)], axis=1)
+
+    def weighted_hist(b, at):
+        return res[:, at] * batch_row(w, b)
+
+    def weighted_fresh(b, at):
+        return jnp.broadcast_to(batch_row(fresh_w, b), (SUBS, width))
+
     def turn(block, by):
         return pltpu.roll(block, by % LANES, 1) if by % LANES else block
 
@@ -298,16 +307,17 @@
             acc = lax.fori_loop(tiles // 16, tiles // 8, gram, acc)
             loads[3].wait()
             loads[4].wait()
-            slot_row = jnp.zeros((1, LANES), F32)
+            id_row = jnp.zeros((1, LANES), F32)
             for b in range(batches):
-                slot_row = jnp.where(lane_row == half + b, owner_slot[batch_atom[b]].astype(F32), slot_row)
-            id_rows[pl.ds(in_sheet, 1)] = slot_row[None]
+                id_row = jnp.where(lane_row == half + b, owner_slot[batch_atom[b]].astype(F32), id_row)
+            id_rows[pl.ds(in_sheet, 1)] = id_row[None]
             packed = jnp.zeros((SUBS, LANES), F32)
             for r in range(shifts):
                 packed = jnp.where(lane == hist_len * r + sub, jnp.sum(acc[r], axis=1, keepdims=True), packed)
-            stack_row[pl.ds(in_stack, 1)] = (jnp.sum(packed, axis=0, keepdims=True) + slot_row)[None]
-            loads[5].wait()
-            weigh()
+            stack_row[pl.ds(in_stack, 1)] = (jnp.sum(packed, axis=0, keepdims=True) + id_row)[None]
+            for load in loads[5:9]:
+                load.wait()
+            weigh(weighted_hist)
             mine = hist_all.at[in_stack]
             for pair in range(hist_len // 2):
                 turned = jnp.concatenate(
@@ -322,19 +332,19 @@
             pl.semaphore_wait(barrier, sum(group[0] - 1 for group in groups))
         else:
             slot = slot_index[iteration - 1]
-            replaced = sub == slot
+            slot_row = jnp.zeros((1, LANES), jnp.int32) + slot
 
             def refresh(step, acc):
+                acc, own = acc
                 for u in range(8):
                     t = step * 8 + u
-                    new_res = jnp.where(replaced, fresh[pl.ds(t, 1), :], res[:, lane_tile(t)])
-                    new_rho = jnp.where(replaced, density_out[pl.ds(t, 1), :], rho[:, lane_tile(t)])
-                    res[:, lane_tile(t)] = new_res
-                    rho[:, lane_tile(t)] = new_rho
-                    acc = acc + fresh_w[pl.ds(t, 1), :] * new_res
-                return acc
-
-            acc = lax.fori_loop(0, tiles // 8, refresh, jnp.zeros((SUBS, LANES), F32))
+                    acc = acc + fresh_w[pl.ds(t, 1), :] * res[:, lane_tile(t)]
+                rows_at = pl.ds(pl.multiple_of(step * 8, 8), 8)
+                return acc, own + fresh_w[rows_at, :] * fresh[rows_at, :]
+
+            zero = jnp.zeros((SUBS, LANES), F32)
+            acc, own = lax.fori_loop(0, tiles // 8, refresh, (zero, zero))
+            acc = jnp.where(sub == slot, jnp.sum(own, axis=0, keepdims=True), acc)
             packed = jnp.where(lane == sub, jnp.sum(acc, axis=1, keepdims=True), 0.0)
             stack_row[pl.ds(in_stack, 1)] = jnp.sum(packed, axis=0, keepdims=True)[None]
         wait = exchange(stack_row, stack_group)
@@ -345,7 +355,6 @@
             passed, across = channel(), channel()
             sibling = stack_peer((0, 1))[1]
             far = planes // 2
-            near_steps = [(sign * hop) % planes for hop in (far // 2, 1) for sign in (1, -1)]
 
             def block_of(step):
                 return hist_all.at[stack_peer((-step % planes, 0))[0]]
@@ -356,38 +365,44 @@
             def landed(block, arrival):
                 pltpu.make_async_copy(block, block, pass_sem.at[arrival]).wait()
 
+            def relay(k):
+                for sign in (1, -1):
+                    block = block_of(sign * hops).at[parts[k]]
+                    landed(block, sign * hops % planes if k else planes + (sign < 0))
+                    if (sign < 0) == bool(k):
+                        move(block, sign * hops, far)
+                    move(block, sign * (far - 1 - hops), sign * (far - 1) % planes)
+                    pass_on(block)
+
             def pass_on(block):
                 copy_to(block, block, passed, sibling).start()
 
-            for step in near_steps:
-                move(mine, step, step)
+            parts = [pl.ds(k * hist_len // 4, hist_len // 4) for k in range(2)]
+            hops = far // 2
+            for k in range(2):
+                for sign in (1, -1):
+                    move(mine.at[parts[k]], sign * hops, sign * hops % planes if k else planes + (sign < 0))
+            for sign in (1, -1):
+                move(mine, sign, sign % planes)
             pass_on(mine)
             drained(hist_all.at[pl.ds(0, planes - 1)], across)
             wait_passed = waiter(hist_all, hist_all, passed, planes)
         else:
-            weigh()
+            weigh(weighted_fresh)
             fresh_rows = hist_moments[0:rows]
-            slot_vec = jnp.zeros((rows, LANES), jnp.int32) + slot
-            for i in range(1, hist_len):
-                fresh_rows = jnp.where(slot_vec == i, hist_moments[i * rows : (i + 1) * rows], fresh_rows)
             turned = jnp.concatenate([turn(fresh_rows, -32 * q - 16 * h) for h in range(2) for q in range(4)], axis=0)
             new_moment = fresh_all.at[iteration - 1]
             new_moment[pl.ds(in_stack, 1)] = jnp.transpose(turned)[0 : 2 * SUBS][None]
             wait_fresh = exchange(new_moment, stack_group)
 
+        if iteration == 0:
+            relay(0)
         wait()
         sheet_row[pl.ds(in_sheet, 1)] = total(stack_row, stack)[None]
         wait = exchange(sheet_row, sheet_group)
 
         if iteration == 0:
-            hops = far // 2
-            for sign in (1, -1):
-                block = block_of(sign * hops)
-                landed(block, sign * hops % planes)
-                part = pl.ds(0 if sign > 0 else hist_len // 4, hist_len // 4)
-                move(block.at[part], sign * hops, far)
-                move(block, sign * (far - 1 - hops), sign * (far - 1) % planes)
-                pass_on(block)
+            relay(1)
 
             ids = jnp.concatenate([stack_row[k] for k in range(stack)] * (LANES // stack), axis=0)
             ids = jnp.transpose(ids)
@@ -414,7 +429,7 @@
                 held = member * owned + ((at // spans) * depth + lax.rem(my_plane, depth)) * share
                 fill(lane_tile(t + near_lanes // LANES), (held + lane_row % share).astype(F32))
 
-            for load in loads[6:]:
+            for load in loads[9:]:
                 load.wait()
 
         wait()
@@ -428,18 +443,14 @@
                     entry[i][j] = splat(row, at)
         else:
             news = [splat(row, k) for k in range(hist_len)]
-            slot_vec = jnp.zeros((1, LANES), jnp.int32) + slot
             entry = [
                 [
-                    jnp.where(slot_vec == i, news[j], jnp.where(slot_vec == j, news[i], entry[i][j]))
+                    jnp.where(slot_row == i, news[j], jnp.where(slot_row == j, news[i], entry[i][j]))
                     for j in range(i + 1)
                 ]
                 for i in range(hist_len)
             ]
         coeffs = solve_coeffs(entry, hist_len)
-        coeff_col = jnp.zeros((SUBS, LANES), F32)
-        for i in range(hist_len):
-            coeff_col = jnp.where(sub == i, coeffs[i], coeff_col)
 
         if iteration == 0:
             for step in (1, planes - 1, far - 1, planes - far + 1, far):
@@ -450,10 +461,14 @@
             old = coeffs
         else:
             wait_fresh()
-            old = [jnp.where(slot_vec == i, 0.0, coeffs[i]) for i in range(hist_len)]
+            old = [jnp.where(slot_row == i, 0.0, coeffs[i]) for i in range(hist_len)]
             new = coeffs[0]
             for i in range(1, hist_len):
-                new = jnp.where(slot_vec == i, coeffs[i], new)
+                new = jnp.where(slot_row == i, coeffs[i], new)
+
+        coeff_col = jnp.zeros((SUBS, LANES), F32)
+        for i in range(hist_len):
+            coeff_col = jnp.where(sub == i, old[i], coeff_col)
 
         gains = [jnp.where(low_row, old[2 * pair], old[2 * pair + 1]) for pair in range(hist_len // 2)]
 
@@ -547,6 +562,8 @@
 
         lax.fori_loop(0, batches // 16, density_step, damped)
         density = base_rows[...] - correct[...]
+        if iteration:
+            density = density + new * (density_out[...] + mixing_beta * fresh[...])
         density_out[...] = density
         if last:
             wait_chunks()
@@ -560,9 +577,9 @@
                     top = min(SUBS, harmonics - g * SUBS)
                     moments_out[g * SUBS : g * SUBS + top, t * LANES : (t + 1) * LANES] = tile[0:top]
         else:
-            new = target[...] + coupling[...] * jnp.tanh(density) - density
-            fresh[...] = new
-            fresh_w[...] = new * w[...]
+            made = target[...] + coupling[...] * jnp.tanh(density) - density
+            fresh[...] = made
+            fresh_w[...] = made * w[...]
     for src, sem in sends:
         pltpu.make_async_copy(src, src, sem).wait()
 
@@ -624,10 +641,10 @@
             pltpu.SMEM(batch_atom.shape, jnp.int32),
             pltpu.SMEM(owner_slot.shape, jnp.int32),
             pltpu.SMEM(slot_index.shape, jnp.int32),
-            pltpu.SemaphoreType.DMA((10,)),
+            pltpu.SemaphoreType.DMA((13,)),
             pltpu.SemaphoreType.DMA((kinds,)),
             pltpu.SemaphoreType.DMA((kinds,)),
-            pltpu.SemaphoreType.DMA((planes,)),
+            pltpu.SemaphoreType.DMA((planes + 2,)),
         ],
         compiler_params=pltpu.CompilerParams(
             collective_id=0, has_side_effects=True, vmem_limit_bytes=16777216

time: 47.5 us -> 46.4 us (0.977)
  Pallas kernels: 46.8 us -> 45.7 us
    pallas_call x1, Pallas kernels: 46.1 us -> 45 us  [local(): pl.pallas_call(functools.partial(kernel, cfg), out_shape=(jax.ShapeDtypeS...]
where the time goes in v6:
time: 46.4 us; the launch traced here: 46.3 us
  Pallas kernels  45.7 us (98%)
  between operations  0.64 us (1%)
    pallas_call x1, Pallas kernels, local(): pl.pallas_call(functools.partial(kernel, cfg), out_shape=(jax.ShapeDtypeS...  45 us

profile of v6, /device:TPU:2, one launch (start us, length us, event | category | flops | bytes accessed | tf_op | source)
XLA Modules:
  0.0 46.3 jit_solution(1174834058227491029)
XLA Ops:
  0.6 45.0 %shard_map.104 = (f32[128,128]{1,0:T(8,128)S(1)}, f32[25,512]{1,0:T(8,128)S(1)}) custom-call(s32[64]{0:T(128)} %batch_atom_hbm.1, s32[4096]{0:T(1024)} %owner_slot_hbm.1, s32[2]{0:T(128)} %slot_index_hbm.1, f32[128,128]{1,0:T(8,128)} %bitcast.4, f32[128,128]{1,0:T(8,128)} %bitcast.5, f32[128,128]{1,0:T(8,128)} %bitcast.6, f32[25,16384]{1,0:T(8,128)} %basis_hbm.1, ...), custom_call_target="tpu_custom_call" | custom-call | tf_op jit(solution)/shard_map/pallas_call | solution.py:612
  45.7 0.7 %shard_map.105 = (f32[128,128]{1,0:T(8,128)}, f32[25,512]{1,0:T(8,128)}) custom-call(f32[128,128]{1,0:T(8,128)S(1)} %get-tuple-element.6.density, f32[25,512]{1,0:T(8,128)S(1)} %get-tuple-element.7.moments), custom_call_target="tpu_custom_call" | custom-call | tf_op jit(solution)/shard_map/pallas_call | solution.py:668

commit v7 on v6

--- a/solution.py
+++ b/solution.py
@@ -84,6 +84,9 @@
     part_recv,
     own_send,
     own_recv,
+    old_send,
+    old_recv,
+    old_pieces,
     chunks,
     source_cols,
     mask,
@@ -278,6 +281,32 @@
     def turn(block, by):
         return pltpu.roll(block, by % LANES, 1) if by % LANES else block
 
+    def unfold(one, two):
+        upper = jnp.where(low, one, pltpu.roll(two, half, 1))
+        lower = jnp.where(low, pltpu.roll(one, half, 1), two)
+        return jnp.concatenate([upper, lower], axis=0)
+
+    def in_pieces(blocks):
+        everywhere = jnp.concatenate(blocks, axis=1)
+        return jnp.concatenate(split(everywhere), axis=0).astype(jnp.bfloat16)
+
+    def gathered(pieces, first, count):
+        return jnp.dot(pieces, mask[:, pl.ds(pl.multiple_of(first, count), count)], preferred_element_type=F32)
+
+    def joined(out):
+        return out[0:32] + out[32:64] + out[64:96]
+
+    many = 2 * LANES // share
+    each = LANES // share
+
+    def kept(out, k):
+        tile = out[:, k // each * LANES : (k // each + 1) * LANES]
+        result = jnp.zeros((SUBS, LANES), F32)
+        for g in range(4):
+            piece = tile[g * SUBS : (g + 1) * SUBS]
+            result = jnp.where(quarter == g, turn(piece, (g - k % each) * 32), result)
+        return result
+
     shifts = hist_len // 2 + 1
     entry = None
     for iteration in range(iters):
@@ -432,6 +461,21 @@
             for load in loads[9:]:
                 load.wait()
 
+        if iteration:
+            wait_fresh()
+            fresh_blocks = [unfold(new_moment[k], new_moment[k + 1]) for k in range(0, stack, 2)]
+            pieces = in_pieces(fresh_blocks)
+            send, wait_own = scatter(own_send, own_recv, sheet_group)
+            for first in range(0, sheet, many):
+                out = joined(gathered(pieces, near_lanes + first * share, many * share))
+                for k in range(many):
+                    own_send[first + k] = kept(out, k)
+            own_recv[pl.ds(in_sheet, 1)] = own_send[pl.ds(in_sheet, 1)]
+            for step in sheet_group[3]:
+                send(step)
+            wait_old()
+            held_old = [tree(old_recv[k, i] for k in range(sheet)) for i in range(hist_len)]
+
         wait()
         row = total(sheet_row, sheet)
         if iteration == 0:
@@ -460,7 +504,6 @@
             wait_passed()
             old = coeffs
         else:
-            wait_fresh()
             old = [jnp.where(slot_row == i, 0.0, coeffs[i]) for i in range(hist_len)]
             new = coeffs[0]
             for i in range(1, hist_len):
@@ -483,40 +526,14 @@
             block = jnp.where(low_wide, one, two) + pltpu.roll(jnp.where(low_wide, two, one), half, 1)
             if iteration:
                 one, two = new_moment[k], new_moment[k + 1]
-                upper = jnp.where(low, one, pltpu.roll(two, half, 1))
-                lower = jnp.where(low, pltpu.roll(one, half, 1), two)
-                block = block + new * jnp.concatenate([upper, lower], axis=0)
+                block = block + new * unfold(one, two)
             blocks.append(block)
-        everywhere = jnp.concatenate(blocks, axis=1)
-        pieces = jnp.concatenate(split(everywhere), axis=0).astype(jnp.bfloat16)
-
-        def gathered(first, count):
-            out = jnp.dot(
-                pieces, mask[:, pl.ds(pl.multiple_of(first, count), count)], preferred_element_type=F32
-            )
-            return out[0:32] + out[32:64] + out[64:96]
-
-        if last:
-            many = 2 * LANES // share
-            each = LANES // share
-            send, wait_own = scatter(own_send, own_recv, sheet_group)
-            for first in range(0, sheet, many):
-                out = gathered(near_lanes + first * share, many * share)
-                for k in range(many):
-                    tile = out[:, k // each * LANES : (k // each + 1) * LANES]
-                    kept = jnp.zeros((SUBS, LANES), F32)
-                    for g in range(4):
-                        piece = tile[g * SUBS : (g + 1) * SUBS]
-                        kept = jnp.where(quarter == g, turn(piece, (g - k % each) * 32), kept)
-                    own_send[first + k] = kept
-            own_recv[pl.ds(in_sheet, 1)] = own_send[pl.ds(in_sheet, 1)]
-            for step in sheet_group[3]:
-                send(step)
+        pieces = in_pieces(blocks)
 
         send, wait = scatter(sent, received, sheet_group)
         for line_step in sorted(range(lines), key=lambda step: -ring(step, lines)):
             first = lax.rem(my_line + line_step, lines) * spans
-            out = gathered(first * batches, spans * batches)
+            out = joined(gathered(pieces, first * batches, spans * batches))
             for k in range(0, spans, 2):
                 upper = out[0:16, k * batches : (k + 2) * batches]
                 lower = out[16:32, k * batches : (k + 2) * batches]
@@ -536,9 +553,35 @@
 
         lax.fori_loop(0, tiles // 8, base_step, 0)
 
+        if iteration == 0:
+            @pl.loop(0, hist_len // 2)
+            def _(pair):
+                ones = [hist_all[k, pair, 0:24] for k in range(stack)]
+                ends = [jnp.broadcast_to(hist_all[k, pair, 24:25], (SUBS, LANES)) for k in range(stack)]
+                rows_of = [jnp.concatenate([ones[k], ends[k]], axis=0) for k in range(stack)]
+                firsts, seconds = [], []
+                for k in range(0, stack, 2):
+                    one, two = rows_of[k], rows_of[k + 1]
+                    firsts.append(jnp.where(low_wide, one, pltpu.roll(two, half, 1)))
+                    seconds.append(jnp.where(low_wide, pltpu.roll(one, half, 1), two))
+                old_pieces[pl.ds(pl.multiple_of(pair * 192, 192), 96)] = in_pieces(firsts)
+                old_pieces[pl.ds(pl.multiple_of(pair * 192 + 96, 96), 96)] = in_pieces(seconds)
+
+            send, wait_old = scatter(old_send, old_recv, sheet_group)
+            for first in range(0, sheet, many):
+                out = gathered(old_pieces[...], near_lanes + first * share, many * share)
+                for i in range(hist_len):
+                    part = joined(out[i * 96 : (i + 1) * 96])
+                    for k in range(many):
+                        old_send[first + k, i] = kept(part, k)
+            old_recv[pl.ds(in_sheet, 1)] = old_send[pl.ds(in_sheet, 1)]
+            for step in sheet_group[3]:
+                send(step)
+
         if last:
             wait_own()
-            chunks[pl.ds(my_share, 1)] = (total(own_recv, sheet) * scale)[None]
+            held = new * total(own_recv, sheet) + tree(old[i] * held_old[i] for i in range(hist_len))
+            chunks[pl.ds(my_share, 1)] = (held * scale)[None]
             wait_chunks = exchange(chunks, share_group)
 
         wait()
@@ -567,7 +610,6 @@
         density_out[...] = density
         if last:
             wait_chunks()
-            each = LANES // share
             for t in range(owned // LANES):
                 held = [chunks[t * each + k] for k in range(each)]
                 for g in range(4):
@@ -606,7 +648,7 @@
     cfg = (iters, hist_len, harmonics, batches, points // batches, owned, planes, lines, spans, cores, scale)
     tiles = points // LANES
     flat = (tiles, LANES)
-    kinds = 3 * iters + 5 + (iters - 1)
+    kinds = 3 * iters + 6 + (iters - 1)
     any_space = pl.BlockSpec(memory_space=pltpu.HBM)
     vmem = pl.BlockSpec(memory_space=pltpu.VMEM)
     density, moments = pl.pallas_call(
@@ -632,6 +674,9 @@
             pltpu.VMEM((iters, sheet, 2 * SUBS, LANES), F32),
             pltpu.VMEM((sheet, SUBS, LANES), F32),
             pltpu.VMEM((sheet, SUBS, LANES), F32),
+            pltpu.VMEM((sheet, hist_len, SUBS, LANES), F32),
+            pltpu.VMEM((sheet, hist_len, SUBS, LANES), F32),
+            pltpu.VMEM((hist_len * 96, stack * batches), jnp.bfloat16),
             pltpu.VMEM((shares, SUBS, LANES), F32),
             pltpu.VMEM((stack * batches, LANES), F32),
             pltpu.VMEM((stack * batches, sheet * (batches + owned // shares)), jnp.bfloat16),

time: 46.4 us -> 44.6 us (0.961)
  Pallas kernels: 45.7 us -> 43.8 us
    pallas_call x1, Pallas kernels: 45 us -> 43.1 us  [local(): pl.pallas_call(functools.partial(kernel, cfg), out_shape=(jax.ShapeDtypeS...]
where the time goes in v7:
time: 44.6 us; the launch traced here: 44.4 us
  Pallas kernels  43.8 us (98%)
  between operations  0.64 us (1%)
    pallas_call x1, Pallas kernels, local(): pl.pallas_call(functools.partial(kernel, cfg), out_shape=(jax.ShapeDtypeS...  43.1 us

profile of v7, /device:TPU:2, one launch (start us, length us, event | category | flops | bytes accessed | tf_op | source)
XLA Modules:
  0.0 44.4 jit_solution(10758467654469088165)
XLA Ops:
  0.6 43.1 %shard_map.104 = (f32[128,128]{1,0:T(8,128)S(1)}, f32[25,512]{1,0:T(8,128)S(1)}) custom-call(s32[64]{0:T(128)} %batch_atom_hbm.1, s32[4096]{0:T(1024)} %owner_slot_hbm.1, s32[2]{0:T(128)} %slot_index_hbm.1, f32[128,128]{1,0:T(8,128)} %bitcast.4, f32[128,128]{1,0:T(8,128)} %bitcast.5, f32[128,128]{1,0:T(8,128)} %bitcast.6, f32[25,16384]{1,0:T(8,128)} %basis_hbm.1, ...), custom_call_target="tpu_custom_call" | custom-call | tf_op jit(solution)/shard_map/pallas_call | solution.py:654
  43.8 0.7 %shard_map.105 = (f32[128,128]{1,0:T(8,128)}, f32[25,512]{1,0:T(8,128)}) custom-call(f32[128,128]{1,0:T(8,128)S(1)} %get-tuple-element.6.density, f32[25,512]{1,0:T(8,128)S(1)} %get-tuple-element.7.moments), custom_call_target="tpu_custom_call" | custom-call | tf_op jit(solution)/shard_map/pallas_call | solution.py:713

commit v8 on v7

--- a/solution.py
+++ b/solution.py
@@ -87,8 +87,12 @@
     old_send,
     old_recv,
     old_pieces,
+    basis_pieces,
+    early_sum,
+    near_sum,
     chunks,
     source_cols,
+    near_cols,
     mask,
     hist_moments,
     base_rows,
@@ -146,6 +150,10 @@
     sheet_group = (sheet, in_sheet, sheet_peer, far_first(lines, spans))
     share_group = (shares, my_share, share_peer, far_first(lines, depth))
     groups = (stack_group, sheet_group)
+    far = planes // 2
+    arrivals = [0, 1, -1] + [sign * hop for hop in range(2, far) for sign in (1, -1)] + [far]
+    sources = [stack_peer((offset % planes, core))[0] for offset in arrivals for core in range(cores)]
+    early = (2 * far - 3) * cores
     barrier = pltpu.get_barrier_semaphore()
     for _, _, peer, steps in groups:
         for step in steps:
@@ -243,7 +251,7 @@
     def splat(row, k):
         return jnp.broadcast_to(row[:, k : k + 1], (1, LANES))
 
-    def weigh(weighted):
+    def weigh():
         @pl.loop(0, rows // 4)
         def _(step):
             for u in range(4):
@@ -252,16 +260,15 @@
                 for q in range(4):
                     b = q * rows + r
                     at = pl.ds(pl.multiple_of(b * width, width), width)
-                    xs.extend(split(weighted(b, at)))
-                    ys.append(
-                        jnp.concatenate([basis[0:24, at], jnp.broadcast_to(basis[24:25, at], (SUBS, width))], axis=0)
-                    )
+                    xs.extend(split(res[:, at] * batch_row(w, b)))
+                    end = jnp.broadcast_to(basis[24:25, at], (SUBS, width))
+                    ys.append(jnp.concatenate([basis[0:24, at], end], axis=0))
                 x = jnp.concatenate(xs, axis=0).astype(jnp.bfloat16)
                 out = None
-                for y in split(jnp.concatenate(ys, axis=0), 2):
-                    part = lax.dot_general(
-                        x, y.astype(jnp.bfloat16), (((1,), (1,)), ((), ())), preferred_element_type=F32
-                    )
+                for k, y in enumerate(split(jnp.concatenate(ys, axis=0), 2)):
+                    y = y.astype(jnp.bfloat16)
+                    basis_pieces[k, pl.ds(pl.multiple_of(r * LANES, LANES), LANES)] = y
+                    part = lax.dot_general(x, y, (((1,), (1,)), ((), ())), preferred_element_type=F32)
                     out = part if out is None else out + part
                 tile = jnp.zeros((SUBS, LANES), F32)
                 for q in range(4):
@@ -269,14 +276,27 @@
                     tile = jnp.where(quarter == q, block, tile)
                 hist_moments[pl.ds(r, hist_len, stride=rows), :] = tile
 
+    def weigh_fresh():
+        x = jnp.concatenate([fresh_w[pl.ds(v, batches, stride=per_batch), :] for v in range(per_batch)], axis=1)
+        x = jnp.concatenate(split(x), axis=0).astype(jnp.bfloat16)
+        out = None
+        for k in range(2):
+            part = lax.dot_general(x, basis_pieces[k], (((1,), (1,)), ((), ())), preferred_element_type=F32)
+            out = part if out is None else out + part
+        made = []
+        for first in range(0, rows, SUBS):
+            block = jnp.zeros((SUBS, LANES), F32)
+            for u in range(SUBS):
+                tile = slice((first + u) * LANES, (first + u + 1) * LANES)
+                for q in range(4):
+                    at = [k * batches + q * rows + first for k in range(3)]
+                    piece = tree(out[begin : begin + SUBS, tile] for begin in at)
+                    block = jnp.where((sub == u) & (quarter == q), piece, block)
+            made.append(block)
+        return jnp.concatenate(made, axis=0)
+
     def batch_row(ref, b):
         return jnp.concatenate([ref[pl.ds(b * per_batch + v, 1), :] for v in range(per_batch)], axis=1)
-
-    def weighted_hist(b, at):
-        return res[:, at] * batch_row(w, b)
-
-    def weighted_fresh(b, at):
-        return jnp.broadcast_to(batch_row(fresh_w, b), (SUBS, width))
 
     def turn(block, by):
         return pltpu.roll(block, by % LANES, 1) if by % LANES else block
@@ -346,7 +366,7 @@
             stack_row[pl.ds(in_stack, 1)] = (jnp.sum(packed, axis=0, keepdims=True) + id_row)[None]
             for load in loads[5:9]:
                 load.wait()
-            weigh(weighted_hist)
+            weigh()
             mine = hist_all.at[in_stack]
             for pair in range(hist_len // 2):
                 turned = jnp.concatenate(
@@ -381,9 +401,8 @@
             wait_ids = exchange(id_rows, sheet_group)
 
         if iteration == 0:
-            passed, across = channel(), channel()
+            passed, passed_late, across = channel(), channel(), channel()
             sibling = stack_peer((0, 1))[1]
-            far = planes // 2
 
             def block_of(step):
                 return hist_all.at[stack_peer((-step % planes, 0))[0]]
@@ -403,8 +422,8 @@
                     move(block, sign * (far - 1 - hops), sign * (far - 1) % planes)
                     pass_on(block)
 
-            def pass_on(block):
-                copy_to(block, block, passed, sibling).start()
+            def pass_on(block, late=False):
+                copy_to(block, block, passed_late if late else passed, sibling).start()
 
             parts = [pl.ds(k * hist_len // 4, hist_len // 4) for k in range(2)]
             hops = far // 2
@@ -415,10 +434,10 @@
                 move(mine, sign, sign % planes)
             pass_on(mine)
             drained(hist_all.at[pl.ds(0, planes - 1)], across)
-            wait_passed = waiter(hist_all, hist_all, passed, planes)
+            wait_passed = waiter(hist_all, hist_all, passed, early // cores)
+            wait_late = waiter(hist_all, hist_all, passed_late, planes - early // cores)
         else:
-            weigh(weighted_fresh)
-            fresh_rows = hist_moments[0:rows]
+            fresh_rows = weigh_fresh()
             turned = jnp.concatenate([turn(fresh_rows, -32 * q - 16 * h) for h in range(2) for q in range(4)], axis=0)
             new_moment = fresh_all.at[iteration - 1]
             new_moment[pl.ds(in_stack, 1)] = jnp.transpose(turned)[0 : 2 * SUBS][None]
@@ -433,30 +452,30 @@
         if iteration == 0:
             relay(1)
 
-            ids = jnp.concatenate([stack_row[k] for k in range(stack)] * (LANES // stack), axis=0)
-            ids = jnp.transpose(ids)
-            for k in range(stack):
-                source_cols[k * batches : (k + 1) * batches] = jnp.broadcast_to(
-                    ids[half : half + batches, k : k + 1], (batches, LANES)
-                )
+            for cols, order in ((source_cols, range(stack)), (near_cols, sources)):
+                ids = jnp.transpose(jnp.concatenate([stack_row[k] for k in order] * (LANES // stack), axis=0))
+                for k in range(stack):
+                    cols[k * batches : (k + 1) * batches] = jnp.broadcast_to(
+                        ids[half : half + batches, k : k + 1], (batches, LANES)
+                    )
             wait_ids()
 
-            def fill(lanes, wanted):
+            def fill(cols, lanes, wanted):
                 for k in range(mask.shape[0] // (2 * SUBS)):
                     at = slice(2 * SUBS * k, 2 * SUBS * (k + 1))
-                    mask[at, lanes] = jnp.where(source_cols[at] == wanted, 1.0, 0.0).astype(jnp.bfloat16)
+                    mask[at, lanes] = jnp.where(cols[at] == wanted, 1.0, 0.0).astype(jnp.bfloat16)
 
             @pl.loop(0, near_lanes // LANES)
             def _(t):
                 pair = jnp.where(low_row, pltpu.roll(id_rows[2 * t], half, 1), id_rows[2 * t + 1])
-                fill(lane_tile(t), pair)
+                fill(near_cols, lane_tile(t), pair)
 
             @pl.loop(0, sheet * share // LANES)
             def _(t):
                 at = t * (LANES // share) + lane_row // share
                 member = (at % spans) * cores + my_core
                 held = member * owned + ((at // spans) * depth + lax.rem(my_plane, depth)) * share
-                fill(lane_tile(t + near_lanes // LANES), (held + lane_row % share).astype(F32))
+                fill(source_cols, lane_tile(t + near_lanes // LANES), (held + lane_row % share).astype(F32))
 
             for load in loads[9:]:
                 load.wait()
@@ -466,16 +485,20 @@
             fresh_blocks = [unfold(new_moment[k], new_moment[k + 1]) for k in range(0, stack, 2)]
             pieces = in_pieces(fresh_blocks)
             send, wait_own = scatter(own_send, own_recv, sheet_group)
-            for first in range(0, sheet, many):
-                out = joined(gathered(pieces, near_lanes + first * share, many * share))
-                for k in range(many):
-                    own_send[first + k] = kept(out, k)
+            out = joined(gathered(pieces, near_lanes, sheet * share))
+            for k in range(sheet):
+                own_send[k] = kept(out, k)
             own_recv[pl.ds(in_sheet, 1)] = own_send[pl.ds(in_sheet, 1)]
             for step in sheet_group[3]:
                 send(step)
             wait_old()
             held_old = [tree(old_recv[k, i] for k in range(sheet)) for i in range(hist_len)]
 
+        if iteration == 0:
+            for step in (1, planes - 1, far - 1, planes - far + 1, far):
+                block = block_of(step)
+                landed(block, step)
+                pass_on(block, step not in (1, planes - 1))
         wait()
         row = total(sheet_row, sheet)
         if iteration == 0:
@@ -497,10 +520,6 @@
         coeffs = solve_coeffs(entry, hist_len)
 
         if iteration == 0:
-            for step in (1, planes - 1, far - 1, planes - far + 1, far):
-                block = block_of(step)
-                landed(block, step)
-                pass_on(block)
             wait_passed()
             old = coeffs
         else:
@@ -520,20 +539,36 @@
             end = tree(gains[pair] * hist_all[at, pair, 24:25] for pair in range(hist_len // 2))
             return jnp.concatenate([top, jnp.broadcast_to(end, (SUBS, LANES))], axis=0)
 
-        blocks = []
-        for k in range(0, stack, 2):
-            one, two = mixed(k), mixed(k + 1)
-            block = jnp.where(low_wide, one, two) + pltpu.roll(jnp.where(low_wide, two, one), half, 1)
-            if iteration:
-                one, two = new_moment[k], new_moment[k + 1]
-                block = block + new * unfold(one, two)
-            blocks.append(block)
-        pieces = in_pieces(blocks)
+        def near_pieces(order):
+            blocks = []
+            for k in range(0, len(order), 2):
+                one, two = mixed(order[k]), mixed(order[k + 1])
+                block = jnp.where(low_wide, one, two) + pltpu.roll(jnp.where(low_wide, two, one), half, 1)
+                if iteration:
+                    block = block + new * unfold(new_moment[order[k]], new_moment[order[k + 1]])
+                blocks.append(block)
+            return in_pieces(blocks)
+
+        split_at = 0 if iteration else early
+        if split_at:
+            early_sum[...] = jnp.dot(
+                near_pieces(sources[:split_at]),
+                mask[0 : split_at * batches, 0:near_lanes],
+                preferred_element_type=F32,
+            )
+            wait_late()
+        out = jnp.dot(
+            near_pieces(sources[split_at:]),
+            mask[split_at * batches :, 0:near_lanes],
+            preferred_element_type=F32,
+        )
+        near_sum[...] = joined(out + early_sum[...] if split_at else out)
 
         send, wait = scatter(sent, received, sheet_group)
         for line_step in sorted(range(lines), key=lambda step: -ring(step, lines)):
             first = lax.rem(my_line + line_step, lines) * spans
-            out = joined(gathered(pieces, first * batches, spans * batches))
+            lanes = pl.ds(pl.multiple_of(first * batches, spans * batches), spans * batches)
+            out = near_sum[:, lanes]
             for k in range(0, spans, 2):
                 upper = out[0:16, k * batches : (k + 2) * batches]
                 lower = out[16:32, k * batches : (k + 2) * batches]
@@ -648,7 +683,7 @@
     cfg = (iters, hist_len, harmonics, batches, points // batches, owned, planes, lines, spans, cores, scale)
     tiles = points // LANES
     flat = (tiles, LANES)
-    kinds = 3 * iters + 6 + (iters - 1)
+    kinds = 3 * iters + 7 + (iters - 1)
     any_space = pl.BlockSpec(memory_space=pltpu.HBM)
     vmem = pl.BlockSpec(memory_space=pltpu.VMEM)
     density, moments = pl.pallas_call(
@@ -677,7 +712,11 @@
             pltpu.VMEM((sheet, hist_len, SUBS, LANES), F32),
             pltpu.VMEM((sheet, hist_len, SUBS, LANES), F32),
             pltpu.VMEM((hist_len * 96, stack * batches), jnp.bfloat16),
+            pltpu.VMEM((2, batches // 4 * LANES, points // batches), jnp.bfloat16),
+            pltpu.VMEM((96, sheet * batches), F32),
+            pltpu.VMEM((32, sheet * batches), F32),
             pltpu.VMEM((shares, SUBS, LANES), F32),
+            pltpu.VMEM((stack * batches, LANES), F32),
             pltpu.VMEM((stack * batches, LANES), F32),
             pltpu.VMEM((stack * batches, sheet * (batches + owned // shares)), jnp.bfloat16),
             pltpu.VMEM((batches // 4 * hist_len, LANES), F32),

time: 44.6 us -> 44 us (0.987)
  Pallas kernels: 43.8 us -> 43.3 us
    pallas_call x1, Pallas kernels: 43.1 us -> 42.6 us  [local(): pl.pallas_call(functools.partial(kernel, cfg), out_shape=(jax.ShapeDtypeS...]
where the time goes in v8:
time: 44 us; the launch traced here: 43.9 us
  Pallas kernels  43.3 us (98%)
  between operations  0.64 us (1%)
    pallas_call x1, Pallas kernels, local(): pl.pallas_call(functools.partial(kernel, cfg), out_shape=(jax.ShapeDtypeS...  42.6 us

profile of v8, /device:TPU:2, one launch (start us, length us, event | category | flops | bytes accessed | tf_op | source)
XLA Modules:
  0.0 43.9 jit_solution(7467518114656886771)
XLA Ops:
  0.6 42.6 %shard_map.104 = (f32[128,128]{1,0:T(8,128)S(1)}, f32[25,512]{1,0:T(8,128)S(1)}) custom-call(s32[64]{0:T(128)} %batch_atom_hbm.1, s32[4096]{0:T(1024)} %owner_slot_hbm.1, s32[2]{0:T(128)} %slot_index_hbm.1, f32[128,128]{1,0:T(8,128)} %bitcast.4, f32[128,128]{1,0:T(8,128)} %bitcast.5, f32[128,128]{1,0:T(8,128)} %bitcast.6, f32[25,16384]{1,0:T(8,128)} %basis_hbm.1, ...), custom_call_target="tpu_custom_call" | custom-call | tf_op jit(solution)/shard_map/pallas_call | solution.py:689
  43.2 0.7 %shard_map.105 = (f32[128,128]{1,0:T(8,128)}, f32[25,512]{1,0:T(8,128)}) custom-call(f32[128,128]{1,0:T(8,128)S(1)} %get-tuple-element.6.density, f32[25,512]{1,0:T(8,128)S(1)} %get-tuple-element.7.moments), custom_call_target="tpu_custom_call" | custom-call | tf_op jit(solution)/shard_map/pallas_call | solution.py:752

commit v9 on v8

--- a/solution.py
+++ b/solution.py
@@ -101,6 +101,7 @@
     owner_slot,
     slot_index,
     load_sem,
+    basis_sem,
     send_sem,
     recv_sem,
     pass_sem,
@@ -159,7 +160,6 @@
         for step in steps:
             pl.semaphore_signal(barrier, inc=1, device_id=peer(step)[1], device_id_type=MESH)
 
-    quarters = [pl.ds(k * tiles * LANES // 4, tiles * LANES // 4) for k in range(4)]
     first_half = pl.ds(0, tiles * LANES // 2)
     second_half = pl.ds(tiles * LANES // 2, tiles * LANES // 2)
     loads = [
@@ -171,7 +171,6 @@
                 (res_hbm.at[:, second_half], res.at[:, second_half]),
                 (batch_atom_hbm, batch_atom),
                 (owner_slot_hbm, owner_slot),
-                *((basis_hbm.at[:, part], basis.at[:, part]) for part in quarters),
                 (slot_index_hbm, slot_index),
                 (rho_hbm, rho),
                 (target_hbm, target),
@@ -179,8 +178,11 @@
             )
         )
     ]
-    for load in loads:
+    basis_parts = [pl.ds(k * tiles * LANES // 4, tiles * LANES // 4) for k in range(4)]
+    for load in loads[:5]:
         load.start()
+    for part in basis_parts:
+        pltpu.make_async_copy(basis_hbm.at[:, part], basis.at[:, part], basis_sem).start()
 
     lane = lax.broadcasted_iota(jnp.int32, (SUBS, LANES), 1)
     sub = lax.broadcasted_iota(jnp.int32, (SUBS, LANES), 0)
@@ -243,6 +245,20 @@
         parts = list(parts)
         while len(parts) > 1:
             parts = [parts[k] + parts[k + 1] if k + 1 < len(parts) else parts[k] for k in range(0, len(parts), 2)]
+        return parts[0]
+
+    def column_sums(parts):
+        parts, gap = list(parts), SUBS // 2
+        while gap:
+            keep = sub % (2 * gap) < gap
+            merged = []
+            for one, two in zip(parts[:gap], parts[gap:]):
+                if 2 * gap == SUBS:
+                    merged.append(jnp.where(keep, one, two) + pltpu.roll(jnp.where(keep, two, one), gap, 0))
+                else:
+                    up, down = pltpu.roll(one, SUBS - gap, 0), pltpu.roll(two, gap, 0)
+                    merged.append(jnp.where(keep, one, down) + jnp.where(keep, up, two))
+            parts, gap = merged, gap // 2
         return parts[0]
 
     def total(buf, count):
@@ -302,9 +318,20 @@
         return pltpu.roll(block, by % LANES, 1) if by % LANES else block
 
     def unfold(one, two):
-        upper = jnp.where(low, one, pltpu.roll(two, half, 1))
-        lower = jnp.where(low, pltpu.roll(one, half, 1), two)
-        return jnp.concatenate([upper, lower], axis=0)
+        low_here = low[0 : one.shape[0]]
+        left = jnp.where(low_here, one, pltpu.roll(two, half, 1))
+        right = jnp.where(low_here, pltpu.roll(one, half, 1), two)
+        end = jnp.broadcast_to(right[12:13], (SUBS, LANES))
+        return jnp.concatenate([left[0:8], right[0:8], left[8:12], right[8:12], end], axis=0)
+
+    def fold(block):
+        left = jnp.concatenate([block[0:8], block[16:21]], axis=0)
+        right = jnp.concatenate([block[8:16], block[20:25]], axis=0)
+        low_here = low[0 : left.shape[0]]
+        return (
+            jnp.where(low_here, left, pltpu.roll(right, half, 1)),
+            jnp.where(low_here, pltpu.roll(left, half, 1), right),
+        )
 
     def in_pieces(blocks):
         everywhere = jnp.concatenate(blocks, axis=1)
@@ -364,9 +391,10 @@
             for r in range(shifts):
                 packed = jnp.where(lane == hist_len * r + sub, jnp.sum(acc[r], axis=1, keepdims=True), packed)
             stack_row[pl.ds(in_stack, 1)] = (jnp.sum(packed, axis=0, keepdims=True) + id_row)[None]
-            for load in loads[5:9]:
-                load.wait()
+            pltpu.make_async_copy(basis_hbm, basis, basis_sem).wait()
             weigh()
+            for load in loads[5:]:
+                load.start()
             mine = hist_all.at[in_stack]
             for pair in range(hist_len // 2):
                 turned = jnp.concatenate(
@@ -385,14 +413,17 @@
 
             def refresh(step, acc):
                 acc, own = acc
-                for u in range(8):
-                    t = step * 8 + u
-                    acc = acc + fresh_w[pl.ds(t, 1), :] * res[:, lane_tile(t)]
-                rows_at = pl.ds(pl.multiple_of(step * 8, 8), 8)
-                return acc, own + fresh_w[rows_at, :] * fresh[rows_at, :]
+                sums = [acc] + [jnp.zeros((SUBS, LANES), F32) for _ in range(3)]
+                for u in range(32):
+                    t = step * 32 + u
+                    sums[u % 4] = sums[u % 4] + fresh_w[pl.ds(t, 1), :] * res[:, lane_tile(t)]
+                for u in range(0, 32, SUBS):
+                    at = pl.ds(pl.multiple_of(step * 32 + u, SUBS), SUBS)
+                    own = own + fresh_w[at, :] * fresh[at, :]
+                return tree(sums), own
 
             zero = jnp.zeros((SUBS, LANES), F32)
-            acc, own = lax.fori_loop(0, tiles // 8, refresh, (zero, zero))
+            acc, own = lax.fori_loop(0, tiles // 32, refresh, (zero, zero))
             acc = jnp.where(sub == slot, jnp.sum(own, axis=0, keepdims=True), acc)
             packed = jnp.where(lane == sub, jnp.sum(acc, axis=1, keepdims=True), 0.0)
             stack_row[pl.ds(in_stack, 1)] = jnp.sum(packed, axis=0, keepdims=True)[None]
@@ -438,9 +469,14 @@
             wait_late = waiter(hist_all, hist_all, passed_late, planes - early // cores)
         else:
             fresh_rows = weigh_fresh()
-            turned = jnp.concatenate([turn(fresh_rows, -32 * q - 16 * h) for h in range(2) for q in range(4)], axis=0)
+            first_lanes = lax.broadcasted_iota(jnp.int32, (rows, LANES), 1) < SUBS
+            turned = [
+                jnp.where(first_lanes, turn(fresh_rows, -32 * q - 8 * h), turn(fresh_rows, -32 * q - 8 - 4 * h))
+                for h in range(2)
+                for q in range(4)
+            ]
             new_moment = fresh_all.at[iteration - 1]
-            new_moment[pl.ds(in_stack, 1)] = jnp.transpose(turned)[0 : 2 * SUBS][None]
+            new_moment[pl.ds(in_stack, 1)] = jnp.transpose(jnp.concatenate(turned, axis=0))[0:13][None]
             wait_fresh = exchange(new_moment, stack_group)
 
         if iteration == 0:
@@ -477,7 +513,7 @@
                 held = member * owned + ((at // spans) * depth + lax.rem(my_plane, depth)) * share
                 fill(source_cols, lane_tile(t + near_lanes // LANES), (held + lane_row % share).astype(F32))
 
-            for load in loads[9:]:
+            for load in loads[5:]:
                 load.wait()
 
         if iteration:
@@ -570,20 +606,17 @@
             lanes = pl.ds(pl.multiple_of(first * batches, spans * batches), spans * batches)
             out = near_sum[:, lanes]
             for k in range(0, spans, 2):
-                upper = out[0:16, k * batches : (k + 2) * batches]
-                lower = out[16:32, k * batches : (k + 2) * batches]
-                sent[first + k] = jnp.where(low, upper, pltpu.roll(lower, half, 1))
-                sent[first + k + 1] = jnp.where(low, pltpu.roll(upper, half, 1), lower)
+                pair = fold(out[:, k * batches : (k + 2) * batches])
+                sent[first + k], sent[first + k + 1] = pair
             for step in sheet_group[3]:
                 if step[0] == line_step:
                     send(step)
         received[pl.ds(in_sheet, 1)] = sent[pl.ds(in_sheet, 1)]
 
         def base_step(step, carry):
-            for u in range(8):
-                t = step * 8 + u
-                part = coeff_col * (rho[:, lane_tile(t)] + mixing_beta * res[:, lane_tile(t)])
-                base_rows[pl.ds(t, 1), :] = jnp.sum(part, axis=0, keepdims=True)
+            spans_at = [lane_tile(step * SUBS + u) for u in range(SUBS)]
+            parts = [coeff_col * (rho[:, at] + mixing_beta * res[:, at]) for at in spans_at]
+            base_rows[pl.ds(pl.multiple_of(step * SUBS, SUBS), SUBS), :] = column_sums(parts)
             return carry
 
         lax.fori_loop(0, tiles // 8, base_step, 0)
@@ -621,24 +654,23 @@
 
         wait()
         summed = total(received, sheet)
-        at_batch = jnp.concatenate([summed, pltpu.roll(summed, half, 1)], axis=0) * scale
+        at_batch = unfold(summed, summed) * scale
         comp = lax.broadcasted_iota(jnp.int32, (32, LANES), 0)
         degree = sum((comp >= (l + 1) * (l + 1)).astype(F32) for l in range(4))
         damped = jnp.where(comp < harmonics, at_batch * (mixing_beta / (1.0 + degree)), 0.0)
 
-        def density_step(step, ahead):
-            for u in range(16):
-                b = step * 16 + u
-                col = jnp.broadcast_to(ahead[:, u : u + 1], (32, LANES))
-                for v in range(per_batch):
-                    t = b * per_batch + v
-                    part = col[24:32] * basis[24:25, lane_tile(t)]
-                    for g in range(3):
-                        part = part + col[g * SUBS : (g + 1) * SUBS] * basis[g * SUBS : (g + 1) * SUBS, lane_tile(t)]
-                    correct[pl.ds(t, 1), :] = jnp.sum(part, axis=0, keepdims=True)
-            return pltpu.roll(ahead, LANES - 16, 1)
-
-        lax.fori_loop(0, batches // 16, density_step, damped)
+        parts = []
+        for b in range(batches):
+            col = jnp.broadcast_to(damped[:, b : b + 1], (32, LANES))
+            for t in range(b * per_batch, (b + 1) * per_batch):
+                at = slice(t * LANES, (t + 1) * LANES)
+                part = col[24:32] * basis[24:25, at]
+                for g in range(3):
+                    part = part + col[g * SUBS : (g + 1) * SUBS] * basis[g * SUBS : (g + 1) * SUBS, at]
+                parts.append(part)
+                if len(parts) == SUBS:
+                    correct[t + 1 - SUBS : t + 1] = column_sums(parts)
+                    parts = []
         density = base_rows[...] - correct[...]
         if iteration:
             density = density + new * (density_out[...] + mixing_beta * fresh[...])
@@ -704,9 +736,9 @@
             pltpu.VMEM((iters, sheet, 1, LANES), F32),
             pltpu.VMEM((sheet, 1, LANES), F32),
             pltpu.VMEM((stack, hist_len // 2, harmonics, LANES), F32),
-            pltpu.VMEM((iters - 1, stack, 2 * SUBS, LANES), F32),
-            pltpu.VMEM((iters, sheet, 2 * SUBS, LANES), F32),
-            pltpu.VMEM((iters, sheet, 2 * SUBS, LANES), F32),
+            pltpu.VMEM((iters - 1, stack, 13, LANES), F32),
+            pltpu.VMEM((iters, sheet, 13, LANES), F32),
+            pltpu.VMEM((iters, sheet, 13, LANES), F32),
             pltpu.VMEM((sheet, SUBS, LANES), F32),
             pltpu.VMEM((sheet, SUBS, LANES), F32),
             pltpu.VMEM((sheet, hist_len, SUBS, LANES), F32),
@@ -725,7 +757,8 @@
             pltpu.SMEM(batch_atom.shape, jnp.int32),
             pltpu.SMEM(owner_slot.shape, jnp.int32),
             pltpu.SMEM(slot_index.shape, jnp.int32),
-            pltpu.SemaphoreType.DMA((13,)),
+            pltpu.SemaphoreType.DMA((9,)),
+            pltpu.SemaphoreType.DMA,
             pltpu.SemaphoreType.DMA((kinds,)),
             pltpu.SemaphoreType.DMA((kinds,)),
             pltpu.SemaphoreType.DMA((planes + 2,)),

time: 44 us -> 43.3 us (0.984)
  Pallas kernels: 43.3 us -> 42.5 us
    pallas_call x1, Pallas kernels: 42.6 us -> 41.8 us  [local(): pl.pallas_call(functools.partial(kernel, cfg), out_shape=(jax.ShapeDtypeS...]
where the time goes in v9:
time: 43.3 us; the launch traced here: 43.1 us
  Pallas kernels  42.5 us (98%)
  between operations  0.64 us (1%)
    pallas_call x1, Pallas kernels, local(): pl.pallas_call(functools.partial(kernel, cfg), out_shape=(jax.ShapeDtypeS...  41.8 us

profile of v9, /device:TPU:2, one launch (start us, length us, event | category | flops | bytes accessed | tf_op | source)
XLA Modules:
  0.0 43.1 jit_solution(35994522847176849)
XLA Ops:
  0.6 41.8 %shard_map.104 = (f32[128,128]{1,0:T(8,128)S(1)}, f32[25,512]{1,0:T(8,128)S(1)}) custom-call(s32[64]{0:T(128)} %batch_atom_hbm.1, s32[4096]{0:T(1024)} %owner_slot_hbm.1, s32[2]{0:T(128)} %slot_index_hbm.1, f32[128,128]{1,0:T(8,128)} %bitcast.4, f32[128,128]{1,0:T(8,128)} %bitcast.5, f32[128,128]{1,0:T(8,128)} %bitcast.6, f32[25,16384]{1,0:T(8,128)} %basis_hbm.1, ...), custom_call_target="tpu_custom_call" | custom-call | tf_op jit(solution)/shard_map/pallas_call | solution.py:721
  42.5 0.7 %shard_map.105 = (f32[128,128]{1,0:T(8,128)}, f32[25,512]{1,0:T(8,128)}) custom-call(f32[128,128]{1,0:T(8,128)S(1)} %get-tuple-element.6.density, f32[25,512]{1,0:T(8,128)S(1)} %get-tuple-element.7.moments), custom_call_target="tpu_custom_call" | custom-call | tf_op jit(solution)/shard_map/pallas_call | solution.py:785

commit v10 on v9

--- a/solution.py
+++ b/solution.py
@@ -155,11 +155,6 @@
     arrivals = [0, 1, -1] + [sign * hop for hop in range(2, far) for sign in (1, -1)] + [far]
     sources = [stack_peer((offset % planes, core))[0] for offset in arrivals for core in range(cores)]
     early = (2 * far - 3) * cores
-    barrier = pltpu.get_barrier_semaphore()
-    for _, _, peer, steps in groups:
-        for step in steps:
-            pl.semaphore_signal(barrier, inc=1, device_id=peer(step)[1], device_id_type=MESH)
-
     first_half = pl.ds(0, tiles * LANES // 2)
     second_half = pl.ds(tiles * LANES // 2, tiles * LANES // 2)
     loads = [
@@ -179,7 +174,13 @@
         )
     ]
     basis_parts = [pl.ds(k * tiles * LANES // 4, tiles * LANES // 4) for k in range(4)]
-    for load in loads[:5]:
+    for load in loads[:3]:
+        load.start()
+    barrier = pltpu.get_barrier_semaphore()
+    for _, _, peer, steps in groups:
+        for step in steps:
+            pl.semaphore_signal(barrier, inc=1, device_id=peer(step)[1], device_id_type=MESH)
+    for load in loads[3:5]:
         load.start()
     for part in basis_parts:
         pltpu.make_async_copy(basis_hbm.at[:, part], basis.at[:, part], basis_sem).start()
@@ -395,6 +396,32 @@
             weigh()
             for load in loads[5:]:
                 load.start()
+            pl.semaphore_wait(barrier, sum(group[0] - 1 for group in groups))
+        else:
+            slot = slot_index[iteration - 1]
+            slot_row = jnp.zeros((1, LANES), jnp.int32) + slot
+
+            def refresh(step, acc):
+                acc, own = acc
+                sums = [acc] + [jnp.zeros((SUBS, LANES), F32) for _ in range(3)]
+                for u in range(32):
+                    t = step * 32 + u
+                    sums[u % 4] = sums[u % 4] + fresh_w[pl.ds(t, 1), :] * res[:, lane_tile(t)]
+                for u in range(0, 32, SUBS):
+                    at = pl.ds(pl.multiple_of(step * 32 + u, SUBS), SUBS)
+                    own = own + fresh_w[at, :] * fresh[at, :]
+                return tree(sums), own
+
+            zero = jnp.zeros((SUBS, LANES), F32)
+            acc, own = lax.fori_loop(0, tiles // 32, refresh, (zero, zero))
+            acc = jnp.where(sub == slot, jnp.sum(own, axis=0, keepdims=True), acc)
+            packed = jnp.where(lane == sub, jnp.sum(acc, axis=1, keepdims=True), 0.0)
+            stack_row[pl.ds(in_stack, 1)] = jnp.sum(packed, axis=0, keepdims=True)[None]
+        wait = exchange(stack_row, stack_group)
+        if iteration == 0:
+            wait_ids = exchange(id_rows, sheet_group)
+
+        if iteration == 0:
             mine = hist_all.at[in_stack]
             for pair in range(hist_len // 2):
                 turned = jnp.concatenate(
@@ -406,32 +433,6 @@
                     axis=0,
                 )
                 mine[pair] = jnp.transpose(turned)[0:harmonics]
-            pl.semaphore_wait(barrier, sum(group[0] - 1 for group in groups))
-        else:
-            slot = slot_index[iteration - 1]
-            slot_row = jnp.zeros((1, LANES), jnp.int32) + slot
-
-            def refresh(step, acc):
-                acc, own = acc
-                sums = [acc] + [jnp.zeros((SUBS, LANES), F32) for _ in range(3)]
-                for u in range(32):
-                    t = step * 32 + u
-                    sums[u % 4] = sums[u % 4] + fresh_w[pl.ds(t, 1), :] * res[:, lane_tile(t)]
-                for u in range(0, 32, SUBS):
-                    at = pl.ds(pl.multiple_of(step * 32 + u, SUBS), SUBS)
-                    own = own + fresh_w[at, :] * fresh[at, :]
-                return tree(sums), own
-
-            zero = jnp.zeros((SUBS, LANES), F32)
-            acc, own = lax.fori_loop(0, tiles // 32, refresh, (zero, zero))
-            acc = jnp.where(sub == slot, jnp.sum(own, axis=0, keepdims=True), acc)
-            packed = jnp.where(lane == sub, jnp.sum(acc, axis=1, keepdims=True), 0.0)
-            stack_row[pl.ds(in_stack, 1)] = jnp.sum(packed, axis=0, keepdims=True)[None]
-        wait = exchange(stack_row, stack_group)
-        if iteration == 0:
-            wait_ids = exchange(id_rows, sheet_group)
-
-        if iteration == 0:
             passed, passed_late, across = channel(), channel(), channel()
             sibling = stack_peer((0, 1))[1]
 

time: 43.3 us -> 43.2 us (level)
  no operation moved by 1% of the time
where the time goes in v10:
time: 43.2 us; the launch traced here: 43.1 us
  Pallas kernels  42.4 us (98%)
  between operations  0.64 us (1%)
    pallas_call x1, Pallas kernels, local(): pl.pallas_call(functools.partial(kernel, cfg), out_shape=(jax.ShapeDtypeS...  41.8 us

profile of v10, /device:TPU:2, one launch (start us, length us, event | category | flops | bytes accessed | tf_op | source)
XLA Modules:
  0.0 43.1 jit_solution(6938650763332349792)
XLA Ops:
  0.6 41.8 %shard_map.104 = (f32[128,128]{1,0:T(8,128)S(1)}, f32[25,512]{1,0:T(8,128)S(1)}) custom-call(s32[64]{0:T(128)} %batch_atom_hbm.1, s32[4096]{0:T(1024)} %owner_slot_hbm.1, s32[2]{0:T(128)} %slot_index_hbm.1, f32[128,128]{1,0:T(8,128)} %bitcast.4, f32[128,128]{1,0:T(8,128)} %bitcast.5, f32[128,128]{1,0:T(8,128)} %bitcast.6, f32[25,16384]{1,0:T(8,128)} %basis_hbm.1, ...), custom_call_target="tpu_custom_call" | custom-call | tf_op jit(solution)/shard_map/pallas_call | solution.py:722
  42.4 0.7 %shard_map.105 = (f32[128,128]{1,0:T(8,128)}, f32[25,512]{1,0:T(8,128)}) custom-call(f32[128,128]{1,0:T(8,128)S(1)} %get-tuple-element.6.density, f32[25,512]{1,0:T(8,128)S(1)} %get-tuple-element.7.moments), custom_call_target="tpu_custom_call" | custom-call | tf_op jit(solution)/shard_map/pallas_call | solution.py:786

commit v11 on v10

--- a/solution.py
+++ b/solution.py
@@ -45,7 +45,7 @@
     return [backward[i] / total for i in range(hist_len)]
 
 
-def split(x, count=3):
+def split(x, count=2):
     pieces = []
     for _ in range(count):
         piece = x.astype(jnp.bfloat16).astype(F32)
@@ -282,14 +282,14 @@
                     ys.append(jnp.concatenate([basis[0:24, at], end], axis=0))
                 x = jnp.concatenate(xs, axis=0).astype(jnp.bfloat16)
                 out = None
-                for k, y in enumerate(split(jnp.concatenate(ys, axis=0), 2)):
+                for k, y in enumerate(split(jnp.concatenate(ys, axis=0))):
                     y = y.astype(jnp.bfloat16)
                     basis_pieces[k, pl.ds(pl.multiple_of(r * LANES, LANES), LANES)] = y
                     part = lax.dot_general(x, y, (((1,), (1,)), ((), ())), preferred_element_type=F32)
                     out = part if out is None else out + part
                 tile = jnp.zeros((SUBS, LANES), F32)
                 for q in range(4):
-                    block = out[24 * q : 24 * q + 8] + out[24 * q + 8 : 24 * q + 16] + out[24 * q + 16 : 24 * q + 24]
+                    block = out[16 * q : 16 * q + 8] + out[16 * q + 8 : 16 * q + 16]
                     tile = jnp.where(quarter == q, block, tile)
                 hist_moments[pl.ds(r, hist_len, stride=rows), :] = tile
 
@@ -306,7 +306,7 @@
             for u in range(SUBS):
                 tile = slice((first + u) * LANES, (first + u + 1) * LANES)
                 for q in range(4):
-                    at = [k * batches + q * rows + first for k in range(3)]
+                    at = [k * batches + q * rows + first for k in range(2)]
                     piece = tree(out[begin : begin + SUBS, tile] for begin in at)
                     block = jnp.where((sub == u) & (quarter == q), piece, block)
             made.append(block)
@@ -342,7 +342,7 @@
         return jnp.dot(pieces, mask[:, pl.ds(pl.multiple_of(first, count), count)], preferred_element_type=F32)
 
     def joined(out):
-        return out[0:32] + out[32:64] + out[64:96]
+        return out[0:32] + out[32:64]
 
     many = 2 * LANES // share
     each = LANES // share
@@ -633,14 +633,14 @@
                     one, two = rows_of[k], rows_of[k + 1]
                     firsts.append(jnp.where(low_wide, one, pltpu.roll(two, half, 1)))
                     seconds.append(jnp.where(low_wide, pltpu.roll(one, half, 1), two))
-                old_pieces[pl.ds(pl.multiple_of(pair * 192, 192), 96)] = in_pieces(firsts)
-                old_pieces[pl.ds(pl.multiple_of(pair * 192 + 96, 96), 96)] = in_pieces(seconds)
+                old_pieces[pl.ds(pl.multiple_of(pair * 128, 128), 64)] = in_pieces(firsts)
+                old_pieces[pl.ds(pl.multiple_of(pair * 128 + 64, 64), 64)] = in_pieces(seconds)
 
             send, wait_old = scatter(old_send, old_recv, sheet_group)
             for first in range(0, sheet, many):
                 out = gathered(old_pieces[...], near_lanes + first * share, many * share)
                 for i in range(hist_len):
-                    part = joined(out[i * 96 : (i + 1) * 96])
+                    part = joined(out[i * 64 : (i + 1) * 64])
                     for k in range(many):
                         old_send[first + k, i] = kept(part, k)
             old_recv[pl.ds(in_sheet, 1)] = old_send[pl.ds(in_sheet, 1)]
@@ -744,9 +744,9 @@
             pltpu.VMEM((sheet, SUBS, LANES), F32),
             pltpu.VMEM((sheet, hist_len, SUBS, LANES), F32),
             pltpu.VMEM((sheet, hist_len, SUBS, LANES), F32),
-            pltpu.VMEM((hist_len * 96, stack * batches), jnp.bfloat16),
+            pltpu.VMEM((hist_len * 64, stack * batches), jnp.bfloat16),
             pltpu.VMEM((2, batches // 4 * LANES, points // batches), jnp.bfloat16),
-            pltpu.VMEM((96, sheet * batches), F32),
+            pltpu.VMEM((64, sheet * batches), F32),
             pltpu.VMEM((32, sheet * batches), F32),
             pltpu.VMEM((shares, SUBS, LANES), F32),
             pltpu.VMEM((stack * batches, LANES), F32),

time: 43.2 us -> 43.1 us (level)
  no operation moved by 1% of the time
where the time goes in v11:
time: 43.1 us; the launch traced here: 43 us
  Pallas kernels  42.4 us (98%)
  between operations  0.64 us (1%)
    pallas_call x1, Pallas kernels, local(): pl.pallas_call(functools.partial(kernel, cfg), out_shape=(jax.ShapeDtypeS...  41.7 us

profile of v11, /device:TPU:2, one launch (start us, length us, event | category | flops | bytes accessed | tf_op | source)
XLA Modules:
  0.0 43.0 jit_solution(1402925435074562232)
XLA Ops:
  0.6 41.7 %shard_map.104 = (f32[128,128]{1,0:T(8,128)S(1)}, f32[25,512]{1,0:T(8,128)S(1)}) custom-call(s32[64]{0:T(128)} %batch_atom_hbm.1, s32[4096]{0:T(1024)} %owner_slot_hbm.1, s32[2]{0:T(128)} %slot_index_hbm.1, f32[128,128]{1,0:T(8,128)} %bitcast.4, f32[128,128]{1,0:T(8,128)} %bitcast.5, f32[128,128]{1,0:T(8,128)} %bitcast.6, f32[25,16384]{1,0:T(8,128)} %basis_hbm.1, ...), custom_call_target="tpu_custom_call" | custom-call | tf_op jit(solution)/shard_map/pallas_call | solution.py:722
  42.4 0.7 %shard_map.105 = (f32[128,128]{1,0:T(8,128)}, f32[25,512]{1,0:T(8,128)}) custom-call(f32[128,128]{1,0:T(8,128)S(1)} %get-tuple-element.6.density, f32[25,512]{1,0:T(8,128)S(1)} %get-tuple-element.7.moments), custom_call_target="tpu_custom_call" | custom-call | tf_op jit(solution)/shard_map/pallas_call | solution.py:786
